TPU v7x, 8 devices: a whole 2x2x1 slice. The times are simulated.
8 devices in a mesh: pc: 2 (over z, y), pr: 4 (over x, core).
Axes of the slice: x: 2, y: 2, z: 1, core: 2. Of those that a mesh axis runs over, the one named last changes fastest.
Arguments:
- panel_in: float32 [6144, 16, 128], P('pr', 'pc')
- trail_in: float32 [6144, 4096], P('pr', 'pc')
Outputs:
- output 1: float32 [6144, 16, 128], P('pr', 'pc')
- output 2: float32 [6144, 4096], P('pr', 'pc')
All inputs are finite; a program needn't handle non-finite values.
Results may differ from a plain program's by a relative error of at most 0.001.
Values sent between devices are 32-bit elements.
A program may use at most 1 GiB of HBM per device.

v0:
```python
import jax
import jax.numpy as jnp
from jax import lax
from jax.sharding import PartitionSpec as P

PREC_HIGH = lax.Precision.HIGHEST


def solve_right(l_diag, right_side):
    return lax.linalg.triangular_solve(l_diag, right_side, left_side=False, lower=True, transpose_a=True)


def apply_update(panel_tile, trail_tile, row_panel, col_view, panel_step, row_procs, col_procs):
    local_rows, panel_dev, blk_size = panel_tile.shape
    row_start = ((panel_step + 1) // row_procs) * blk_size
    col_start = (panel_step + 1) // col_procs
    rows_part = row_panel[row_start:]
    if col_start < panel_dev:
        panel_update = jnp.einsum("rc,mbc->rmb", rows_part, col_view[col_start:panel_dev], precision=PREC_HIGH, preferred_element_type=jnp.float32)
        panel_tile = lax.dynamic_update_slice(panel_tile, panel_tile[row_start:, col_start:] - panel_update, (row_start, col_start, 0))
    trail_view = col_view[panel_dev:].reshape(trail_tile.shape[1], blk_size)
    trail_update = lax.dot_general(rows_part, trail_view, (((1,), (1,)), ((), ())), precision=PREC_HIGH, preferred_element_type=jnp.float32)
    trail_tile = lax.dynamic_update_slice(trail_tile, trail_tile[row_start:] - trail_update, (row_start, 0))
    return panel_tile, trail_tile


def solution(mesh):
    row_procs = mesh.shape["pr"]
    col_procs = mesh.shape["pc"]

    def local_part(panel_tile, trail_tile):
        local_rows, panel_dev, blk_size = panel_tile.shape
        row_blocks = local_rows // blk_size
        col_blocks = row_blocks * row_procs // col_procs
        my_row = lax.axis_index("pr")
        my_col = lax.axis_index("pc")
        block_ids = (jnp.arange(row_blocks) * row_procs + my_row)[:, None, None]
        eye_block = jnp.eye(blk_size, dtype=panel_tile.dtype)
        for panel_step in range(panel_dev * col_procs):
            owner_col = panel_step % col_procs
            local_slot = panel_step // col_procs
            owner_row = panel_step % row_procs
            diag_start = (panel_step // row_procs) * blk_size
            column = panel_tile[:, local_slot, :]
            diag_local = column[diag_start:diag_start + blk_size]
            diag_blk = lax.psum(jnp.where(my_row == owner_row, diag_local, 0.0), "pr")
            diag_blk = jnp.where(my_col == owner_col, diag_blk, eye_block)
            l_diag = jnp.linalg.cholesky(diag_blk)
            solved = solve_right(l_diag, column).reshape(row_blocks, blk_size, blk_size)
            below_diag = jnp.where(block_ids > panel_step, solved, 0.0)
            l_col = jnp.where(block_ids == panel_step, l_diag, below_diag).reshape(local_rows, blk_size)
            new_col = jnp.where(my_col == owner_col, l_col, column)
            panel_tile = lax.dynamic_update_slice(panel_tile, new_col[:, None, :], (0, local_slot, 0))
            row_panel = lax.psum(jnp.where(my_col == owner_col, below_diag.reshape(local_rows, blk_size), 0.0), "pc")
            gathered = lax.all_gather(row_panel, "pr", axis=0, tiled=False)
            by_block = gathered.reshape(row_procs, row_blocks, blk_size, blk_size).transpose(1, 0, 2, 3)
            col_view = lax.dynamic_index_in_dim(by_block.reshape(col_blocks, col_procs, blk_size, blk_size), my_col, axis=1, keepdims=False)
            panel_tile, trail_tile = apply_update(panel_tile, trail_tile, row_panel, col_view, panel_step, row_procs, col_procs)
        return panel_tile, trail_tile

    spec_panel = P("pr", "pc", None)
    spec_trail = P("pr", "pc")
    return jax.shard_map(local_part, mesh=mesh, in_specs=(spec_panel, spec_trail), out_specs=(spec_panel, spec_trail), check_vma=False)
```

profile of v0, /device:TPU:4, one launch (start us, length us, event | category | flops | bytes accessed | tf_op | source)
XLA Modules:
  0.0 2025.5 jit_solution(5463792041328755044)
XLA Ops:
  15.4 26.8 %all-reduce.33.cloned.1.call-done = f32[128,128]{0,1:T(8,128)} async-done(((f32[128,128]{0,1:T(8,128)}), f32[128,128]{0,1:T(8,128)}) %all-reduce.33.cloned.1.call-update) | async-done | bytes 65552 | tf_op jit(solution)/shard_map/psum | solution.py:46
  68.2 27.8 %all-reduce.35.cloned.1.call-done = f32[1536,128]{0,1:T(8,128)} async-done(((f32[1536,128]{0,1:T(8,128)}), f32[1536,128]{0,1:T(8,128)}) %all-reduce.35.cloned.1.call-update) | async-done | bytes 786448 | tf_op jit(solution)/shard_map/psum | solution.py:54
  98.8 25.4 %all-gather.33.cloned.1.call-done = f32[6144,128]{0,1:T(8,128)} async-done(((f32[1536,128]{0,1:T(8,128)}), f32[6144,128]{0,1:T(8,128)}) %all-gather.33.cloned.1.call-update) | async-done | bytes 3145744 | tf_op jit(solution)/shard_map/all_gather | solution.py:55
  140.6 25.8 %all-reduce.37.cloned.1.call-done = f32[128,128]{0,1:T(8,128)} async-done(((f32[128,128]{0,1:T(8,128)}), f32[128,128]{0,1:T(8,128)}) %all-reduce.37.cloned.1.call-update) | async-done | bytes 65552 | tf_op jit(solution)/shard_map/psum | solution.py:46
  194.0 27.6 %all-reduce.39.cloned.1.call-done = f32[1536,128]{0,1:T(8,128)} async-done(((f32[1536,128]{0,1:T(8,128)}), f32[1536,128]{0,1:T(8,128)}) %all-reduce.39.cloned.1.call-update) | async-done | bytes 786448 | tf_op jit(solution)/shard_map/psum | solution.py:54
  224.4 25.2 %all-gather.35.cloned.1.call-done = f32[6144,128]{0,1:T(8,128)} async-done(((f32[1536,128]{0,1:T(8,128)}), f32[6144,128]{0,1:T(8,128)}) %all-gather.35.cloned.1.call-update) | async-done | bytes 3145744 | tf_op jit(solution)/shard_map/all_gather | solution.py:55
  265.0 25.5 %all-reduce.41.cloned.1.call-done = f32[128,128]{0,1:T(8,128)} async-done(((f32[128,128]{0,1:T(8,128)}), f32[128,128]{0,1:T(8,128)}) %all-reduce.41.cloned.1.call-update) | async-done | bytes 65552 | tf_op jit(solution)/shard_map/psum | solution.py:46
  318.3 27.8 %all-reduce.43.cloned.1.call-done = f32[1536,128]{0,1:T(8,128)} async-done(((f32[1536,128]{0,1:T(8,128)}), f32[1536,128]{0,1:T(8,128)}) %all-reduce.43.cloned.1.call-update) | async-done | bytes 786448 | tf_op jit(solution)/shard_map/psum | solution.py:54
  346.3 28.0 %all-gather.37.cloned.1.call-done = f32[6144,128]{0,1:T(8,128)} async-done(((f32[1536,128]{0,1:T(8,128)}), f32[6144,128]{0,1:T(8,128)}) %all-gather.37.cloned.1.call-update) | async-done | bytes 3145744 | tf_op jit(solution)/shard_map/all_gather | solution.py:55
  389.5 25.8 %all-reduce.45.cloned.1.call-done = f32[128,128]{0,1:T(8,128)} async-done(((f32[128,128]{0,1:T(8,128)}), f32[128,128]{0,1:T(8,128)}) %all-reduce.45.cloned.1.call-update) | async-done | bytes 65552 | tf_op jit(solution)/shard_map/psum | solution.py:46
  444.7 27.6 %all-reduce.47.cloned.1.call-done = f32[1536,128]{0,1:T(8,128)} async-done(((f32[1536,128]{0,1:T(8,128)}), f32[1536,128]{0,1:T(8,128)}) %all-reduce.47.cloned.1.call-update) | async-done | bytes 786448 | tf_op jit(solution)/shard_map/psum | solution.py:54
  472.4 27.9 %all-gather.39.cloned.1.call-done = f32[6144,128]{0,1:T(8,128)} async-done(((f32[1536,128]{0,1:T(8,128)}), f32[6144,128]{0,1:T(8,128)}) %all-gather.39.cloned.1.call-update) | async-done | bytes 3145744 | tf_op jit(solution)/shard_map/all_gather | solution.py:55
  511.7 25.8 %all-reduce.49.cloned.1.call-done = f32[128,128]{0,1:T(8,128)} async-done(((f32[128,128]{0,1:T(8,128)}), f32[128,128]{0,1:T(8,128)}) %all-reduce.49.cloned.1.call-update) | async-done | bytes 65552 | tf_op jit(solution)/shard_map/psum | solution.py:46
  563.4 27.8 %all-reduce.51.cloned.1.call-done = f32[1536,128]{0,1:T(8,128)} async-done(((f32[1536,128]{0,1:T(8,128)}), f32[1536,128]{0,1:T(8,128)}) %all-reduce.51.cloned.1.call-update) | async-done | bytes 786448 | tf_op jit(solution)/shard_map/psum | solution.py:54
  594.0 25.2 %all-gather.41.cloned.1.call-done = f32[6144,128]{0,1:T(8,128)} async-done(((f32[1536,128]{0,1:T(8,128)}), f32[6144,128]{0,1:T(8,128)}) %all-gather.41.cloned.1.call-update) | async-done | bytes 3145744 | tf_op jit(solution)/shard_map/all_gather | solution.py:55
  630.8 25.5 %all-reduce.53.cloned.1.call-done = f32[128,128]{0,1:T(8,128)} async-done(((f32[128,128]{0,1:T(8,128)}), f32[128,128]{0,1:T(8,128)}) %all-reduce.53.cloned.1.call-update) | async-done | bytes 65552 | tf_op jit(solution)/shard_map/psum | solution.py:46
  684.0 27.6 %all-reduce.55.cloned.1.call-done = f32[1536,128]{0,1:T(8,128)} async-done(((f32[1536,128]{0,1:T(8,128)}), f32[1536,128]{0,1:T(8,128)}) %all-reduce.55.cloned.1.call-update) | async-done | bytes 786448 | tf_op jit(solution)/shard_map/psum | solution.py:54
  714.3 25.2 %all-gather.43.cloned.1.call-done = f32[6144,128]{0,1:T(8,128)} async-done(((f32[1536,128]{0,1:T(8,128)}), f32[6144,128]{0,1:T(8,128)}) %all-gather.43.cloned.1.call-update) | async-done | bytes 3145744 | tf_op jit(solution)/shard_map/all_gather | solution.py:55
  755.9 21.7 %all-reduce.57.cloned.1.call-done = f32[128,128]{0,1:T(8,128)} async-done(((f32[128,128]{0,1:T(8,128)}), f32[128,128]{0,1:T(8,128)}) %all-reduce.57.cloned.1.call-update) | async-done | bytes 65552 | tf_op jit(solution)/shard_map/psum | solution.py:46
  803.6 27.8 %all-reduce.59.cloned.1.call-done = f32[1536,128]{0,1:T(8,128)} async-done(((f32[1536,128]{0,1:T(8,128)}), f32[1536,128]{0,1:T(8,128)}) %all-reduce.59.cloned.1.call-update) | async-done | bytes 786448 | tf_op jit(solution)/shard_map/psum | solution.py:54
  834.2 25.4 %all-gather.45.cloned.1.call-done = f32[6144,128]{0,1:T(8,128)} async-done(((f32[1536,128]{0,1:T(8,128)}), f32[6144,128]{0,1:T(8,128)}) %all-gather.45.cloned.1.call-update) | async-done | bytes 3145744 | tf_op jit(solution)/shard_map/all_gather | solution.py:55
  876.0 21.7 %all-reduce.61.cloned.1.call-done = f32[128,128]{0,1:T(8,128)} async-done(((f32[128,128]{0,1:T(8,128)}), f32[128,128]{0,1:T(8,128)}) %all-reduce.61.cloned.1.call-update) | async-done | bytes 65552 | tf_op jit(solution)/shard_map/psum | solution.py:46
  925.3 27.6 %all-reduce.63.cloned.1.call-done = f32[1536,128]{0,1:T(8,128)} async-done(((f32[1536,128]{0,1:T(8,128)}), f32[1536,128]{0,1:T(8,128)}) %all-reduce.63.cloned.1.call-update) | async-done | bytes 786448 | tf_op jit(solution)/shard_map/psum | solution.py:54
  955.6 25.2 %all-gather.47.cloned.1.call-done = f32[6144,128]{0,1:T(8,128)} async-done(((f32[1536,128]{0,1:T(8,128)}), f32[6144,128]{0,1:T(8,128)}) %all-gather.47.cloned.1.call-update) | async-done | bytes 3145744 | tf_op jit(solution)/shard_map/all_gather | solution.py:55
  992.0 23.8 %all-reduce.65.cloned.1.call-done = f32[128,128]{0,1:T(8,128)} async-done(((f32[128,128]{0,1:T(8,128)}), f32[128,128]{0,1:T(8,128)}) %all-reduce.65.cloned.1.call-update) | async-done | bytes 65552 | tf_op jit(solution)/shard_map/psum | solution.py:46
  1041.9 27.8 %all-reduce.67.cloned.1.call-done = f32[1536,128]{0,1:T(8,128)} async-done(((f32[1536,128]{0,1:T(8,128)}), f32[1536,128]{0,1:T(8,128)}) %all-reduce.67.cloned.1.call-update) | async-done | bytes 786448 | tf_op jit(solution)/shard_map/psum | solution.py:54
  1072.5 25.2 %all-gather.49.cloned.1.call-done = f32[6144,128]{0,1:T(8,128)} async-done(((f32[1536,128]{0,1:T(8,128)}), f32[6144,128]{0,1:T(8,128)}) %all-gather.49.cloned.1.call-update) | async-done | bytes 3145744 | tf_op jit(solution)/shard_map/all_gather | solution.py:55
  1108.6 24.0 %all-reduce.69.cloned.1.call-done = f32[128,128]{0,1:T(8,128)} async-done(((f32[128,128]{0,1:T(8,128)}), f32[128,128]{0,1:T(8,128)}) %all-reduce.69.cloned.1.call-update) | async-done | bytes 65552 | tf_op jit(solution)/shard_map/psum | solution.py:46
  1160.4 27.5 %all-reduce.71.cloned.1.call-done = f32[1536,128]{0,1:T(8,128)} async-done(((f32[1536,128]{0,1:T(8,128)}), f32[1536,128]{0,1:T(8,128)}) %all-reduce.71.cloned.1.call-update) | async-done | bytes 786448 | tf_op jit(solution)/shard_map/psum | solution.py:54
  1190.7 25.2 %all-gather.51.cloned.1.call-done = f32[6144,128]{0,1:T(8,128)} async-done(((f32[1536,128]{0,1:T(8,128)}), f32[6144,128]{0,1:T(8,128)}) %all-gather.51.cloned.1.call-update) | async-done | bytes 3145744 | tf_op jit(solution)/shard_map/all_gather | solution.py:55
  1225.9 24.2 %all-reduce.73.cloned.1.call-done = f32[128,128]{0,1:T(8,128)} async-done(((f32[128,128]{0,1:T(8,128)}), f32[128,128]{0,1:T(8,128)}) %all-reduce.73.cloned.1.call-update) | async-done | bytes 65552 | tf_op jit(solution)/shard_map/psum | solution.py:46
  1276.3 27.9 %all-reduce.75.cloned.1.call-done = f32[1536,128]{0,1:T(8,128)} async-done(((f32[1536,128]{0,1:T(8,128)}), f32[1536,128]{0,1:T(8,128)}) %all-reduce.75.cloned.1.call-update) | async-done | bytes 786448 | tf_op jit(solution)/shard_map/psum | solution.py:54
  1306.9 25.2 %all-gather.53.cloned.1.call-done = f32[6144,128]{0,1:T(8,128)} async-done(((f32[1536,128]{0,1:T(8,128)}), f32[6144,128]{0,1:T(8,128)}) %all-gather.53.cloned.1.call-update) | async-done | bytes 3145744 | tf_op jit(solution)/shard_map/all_gather | solution.py:55
  1342.3 24.0 %all-reduce.77.cloned.1.call-done = f32[128,128]{0,1:T(8,128)} async-done(((f32[128,128]{0,1:T(8,128)}), f32[128,128]{0,1:T(8,128)}) %all-reduce.77.cloned.1.call-update) | async-done | bytes 65552 | tf_op jit(solution)/shard_map/psum | solution.py:46
  1394.0 27.6 %all-reduce.79.cloned.1.call-done = f32[1536,128]{0,1:T(8,128)} async-done(((f32[1536,128]{0,1:T(8,128)}), f32[1536,128]{0,1:T(8,128)}) %all-reduce.79.cloned.1.call-update) | async-done | bytes 786448 | tf_op jit(solution)/shard_map/psum | solution.py:54
  1424.4 25.2 %all-gather.55.cloned.1.call-done = f32[6144,128]{0,1:T(8,128)} async-done(((f32[1536,128]{0,1:T(8,128)}), f32[6144,128]{0,1:T(8,128)}) %all-gather.55.cloned.1.call-update) | async-done | bytes 3145744 | tf_op jit(solution)/shard_map/all_gather | solution.py:55
  1458.3 24.7 %all-reduce.81.cloned.1.call-done = f32[128,128]{0,1:T(8,128)} async-done(((f32[128,128]{0,1:T(8,128)}), f32[128,128]{0,1:T(8,128)}) %all-reduce.81.cloned.1.call-update) | async-done | bytes 65552 | tf_op jit(solution)/shard_map/psum | solution.py:46
  1509.0 27.8 %all-reduce.83.cloned.1.call-done = f32[1536,128]{0,1:T(8,128)} async-done(((f32[1536,128]{0,1:T(8,128)}), f32[1536,128]{0,1:T(8,128)}) %all-reduce.83.cloned.1.call-update) | async-done | bytes 786448 | tf_op jit(solution)/shard_map/psum | solution.py:54
  1573.6 24.6 %all-reduce.85.cloned.1.call-done = f32[128,128]{0,1:T(8,128)} async-done(((f32[128,128]{0,1:T(8,128)}), f32[128,128]{0,1:T(8,128)}) %all-reduce.85.cloned.1.call-update) | async-done | bytes 65552 | tf_op jit(solution)/shard_map/psum | solution.py:46
  1654.0 22.1 %subtract_subtract_fusion = f32[1536,2048]{1,0:T(8,128)} fusion(f32[1536,2048]{1,0:T(8,128)} %fusion.119, f32[1536,2048]{1,0:T(8,128)} %param.6, f32[1536,2048]{1,0:T(8,128)} %fusion.118, f32[1536,128]{0,1:T(8,128)S(1)} %copy-done.9, f32[2048,128]{1,0:T(8,128)S(1)} %bitcast.791), kind=kOutput, calls=%fused_computation | convolution fusion | flops 4841275392 | bytes 52166656 | tf_op jit(solution)/shard_map/dot_general | solution.py:22
  1677.4 14.0 constant_dynamic-update-slice_fusion.11
  1692.7 13.1 constant_dynamic-update-slice_fusion.10
  1718.6 26.0 %all-reduce.89.cloned.1.call-done = f32[128,128]{0,1:T(8,128)} async-done(((f32[128,128]{0,1:T(8,128)}), f32[128,128]{0,1:T(8,128)}) %all-reduce.89.cloned.1.call-update) | async-done | bytes 65552 | tf_op jit(solution)/shard_map/psum | solution.py:46
  1772.5 17.2 constant_dynamic-update-slice_fusion.9
  1800.7 14.0 constant_dynamic-update-slice_fusion.8
  1829.6 13.1 constant_dynamic-update-slice_fusion.6
  1865.2 25.4 %all-reduce.93.cloned.1.call-done = f32[128,128]{0,1:T(8,128)} async-done(((f32[128,128]{0,1:T(8,128)}), f32[128,128]{0,1:T(8,128)}) %all-reduce.93.cloned.1.call-update) | async-done | bytes 65552 | tf_op jit(solution)/shard_map/psum | solution.py:46
  1918.2 15.8 constant_dynamic-update-slice_fusion.4
  (563 shorter events, 835.5 us)
Async XLA Ops:
  7.2 35.1 %all-reduce.33.cloned.1.call-start = ((), (), s32[]{:S(2)}) async-start(), calls=%async_computation | async-start | bytes 131072 | tf_op jit(solution)/shard_map/psum | solution.py:46
  15.3 80.8 %all-reduce.35.cloned.1.call-start = ((), (), s32[]{:S(2)}) async-start(), calls=%async_computation.1 | async-start | bytes 1572864 | tf_op jit(solution)/shard_map/psum | solution.py:54
  68.2 56.0 %all-gather.33.cloned.1.call-start = ((), (), s32[]{:S(2)}) async-start(), calls=%async_computation.32 | async-start | bytes 3932160 | tf_op jit(solution)/shard_map/all_gather | solution.py:55
  96.1 70.3 %all-reduce.37.cloned.1.call-start = ((), (), s32[]{:S(2)}) async-start(), calls=%async_computation.2 | async-start | bytes 131072 | tf_op jit(solution)/shard_map/psum | solution.py:46
  140.3 81.3 %all-reduce.39.cloned.1.call-start = ((), (), s32[]{:S(2)}) async-start(), calls=%async_computation.3 | async-start | bytes 1572864 | tf_op jit(solution)/shard_map/psum | solution.py:54
  194.0 55.6 %all-gather.35.cloned.1.call-start = ((), (), s32[]{:S(2)}) async-start(), calls=%async_computation.33 | async-start | bytes 3932160 | tf_op jit(solution)/shard_map/all_gather | solution.py:55
  221.6 69.0 %all-reduce.41.cloned.1.call-start = ((), (), s32[]{:S(2)}) async-start(), calls=%async_computation.4 | async-start | bytes 131072 | tf_op jit(solution)/shard_map/psum | solution.py:46
  264.5 81.7 %all-reduce.43.cloned.1.call-start = ((), (), s32[]{:S(2)}) async-start(), calls=%async_computation.5 | async-start | bytes 1572864 | tf_op jit(solution)/shard_map/psum | solution.py:54
  318.3 56.0 %all-gather.37.cloned.1.call-start = ((), (), s32[]{:S(2)}) async-start(), calls=%async_computation.34 | async-start | bytes 3932160 | tf_op jit(solution)/shard_map/all_gather | solution.py:55
  346.2 69.1 %all-reduce.45.cloned.1.call-start = ((), (), s32[]{:S(2)}) async-start(), calls=%async_computation.6 | async-start | bytes 131072 | tf_op jit(solution)/shard_map/psum | solution.py:46
  389.2 83.0 %all-reduce.47.cloned.1.call-start = ((), (), s32[]{:S(2)}) async-start(), calls=%async_computation.7 | async-start | bytes 1572864 | tf_op jit(solution)/shard_map/psum | solution.py:54
  444.7 55.6 %all-gather.39.cloned.1.call-start = ((), (), s32[]{:S(2)}) async-start(), calls=%async_computation.35 | async-start | bytes 3932160 | tf_op jit(solution)/shard_map/all_gather | solution.py:55
  472.3 65.1 %all-reduce.49.cloned.1.call-start = ((), (), s32[]{:S(2)}) async-start(), calls=%async_computation.8 | async-start | bytes 131072 | tf_op jit(solution)/shard_map/psum | solution.py:46
  511.3 79.9 %all-reduce.51.cloned.1.call-start = ((), (), s32[]{:S(2)}) async-start(), calls=%async_computation.9 | async-start | bytes 1572864 | tf_op jit(solution)/shard_map/psum | solution.py:54
  563.3 55.9 %all-gather.41.cloned.1.call-start = ((), (), s32[]{:S(2)}) async-start(), calls=%async_computation.36 | async-start | bytes 3932160 | tf_op jit(solution)/shard_map/all_gather | solution.py:55
  591.3 65.1 %all-reduce.53.cloned.1.call-start = ((), (), s32[]{:S(2)}) async-start(), calls=%async_computation.10 | async-start | bytes 131072 | tf_op jit(solution)/shard_map/psum | solution.py:46
  630.3 81.2 %all-reduce.55.cloned.1.call-start = ((), (), s32[]{:S(2)}) async-start(), calls=%async_computation.11 | async-start | bytes 1572864 | tf_op jit(solution)/shard_map/psum | solution.py:54
  683.9 55.6 %all-gather.43.cloned.1.call-start = ((), (), s32[]{:S(2)}) async-start(), calls=%async_computation.37 | async-start | bytes 3932160 | tf_op jit(solution)/shard_map/all_gather | solution.py:55
  711.5 66.1 %all-reduce.57.cloned.1.call-start = ((), (), s32[]{:S(2)}) async-start(), calls=%async_computation.12 | async-start | bytes 131072 | tf_op jit(solution)/shard_map/psum | solution.py:46
  751.6 79.9 %all-reduce.59.cloned.1.call-start = ((), (), s32[]{:S(2)}) async-start(), calls=%async_computation.13 | async-start | bytes 1572864 | tf_op jit(solution)/shard_map/psum | solution.py:54
  803.5 56.0 %all-gather.45.cloned.1.call-start = ((), (), s32[]{:S(2)}) async-start(), calls=%async_computation.38 | async-start | bytes 3932160 | tf_op jit(solution)/shard_map/all_gather | solution.py:55
  831.5 66.2 %all-reduce.61.cloned.1.call-start = ((), (), s32[]{:S(2)}) async-start(), calls=%async_computation.14 | async-start | bytes 131072 | tf_op jit(solution)/shard_map/psum | solution.py:46
  871.6 81.2 %all-reduce.63.cloned.1.call-start = ((), (), s32[]{:S(2)}) async-start(), calls=%async_computation.15 | async-start | bytes 1572864 | tf_op jit(solution)/shard_map/psum | solution.py:54
  925.3 55.6 %all-gather.47.cloned.1.call-start = ((), (), s32[]{:S(2)}) async-start(), calls=%async_computation.39 | async-start | bytes 3932160 | tf_op jit(solution)/shard_map/all_gather | solution.py:55
  952.9 62.9 %all-reduce.65.cloned.1.call-start = ((), (), s32[]{:S(2)}) async-start(), calls=%async_computation.16 | async-start | bytes 131072 | tf_op jit(solution)/shard_map/psum | solution.py:46
  989.8 80.0 %all-reduce.67.cloned.1.call-start = ((), (), s32[]{:S(2)}) async-start(), calls=%async_computation.17 | async-start | bytes 1572864 | tf_op jit(solution)/shard_map/psum | solution.py:54
  1041.8 55.9 %all-gather.49.cloned.1.call-start = ((), (), s32[]{:S(2)}) async-start(), calls=%async_computation.40 | async-start | bytes 3932160 | tf_op jit(solution)/shard_map/all_gather | solution.py:55
  1069.8 62.9 %all-reduce.69.cloned.1.call-start = ((), (), s32[]{:S(2)}) async-start(), calls=%async_computation.18 | async-start | bytes 131072 | tf_op jit(solution)/shard_map/psum | solution.py:46
  1106.6 81.4 %all-reduce.71.cloned.1.call-start = ((), (), s32[]{:S(2)}) async-start(), calls=%async_computation.19 | async-start | bytes 1572864 | tf_op jit(solution)/shard_map/psum | solution.py:54
  1160.4 55.6 %all-gather.51.cloned.1.call-start = ((), (), s32[]{:S(2)}) async-start(), calls=%async_computation.41 | async-start | bytes 3932160 | tf_op jit(solution)/shard_map/all_gather | solution.py:55
  1188.0 62.2 %all-reduce.73.cloned.1.call-start = ((), (), s32[]{:S(2)}) async-start(), calls=%async_computation.20 | async-start | bytes 131072 | tf_op jit(solution)/shard_map/psum | solution.py:46
  1224.1 80.0 %all-reduce.75.cloned.1.call-start = ((), (), s32[]{:S(2)}) async-start(), calls=%async_computation.21 | async-start | bytes 1572864 | tf_op jit(solution)/shard_map/psum | solution.py:54
  1276.2 55.9 %all-gather.53.cloned.1.call-start = ((), (), s32[]{:S(2)}) async-start(), calls=%async_computation.42 | async-start | bytes 3932160 | tf_op jit(solution)/shard_map/all_gather | solution.py:55
  1304.1 62.1 %all-reduce.77.cloned.1.call-start = ((), (), s32[]{:S(2)}) async-start(), calls=%async_computation.22 | async-start | bytes 131072 | tf_op jit(solution)/shard_map/psum | solution.py:46
  1340.2 81.4 %all-reduce.79.cloned.1.call-start = ((), (), s32[]{:S(2)}) async-start(), calls=%async_computation.23 | async-start | bytes 1572864 | tf_op jit(solution)/shard_map/psum | solution.py:54
  1394.0 55.6 %all-gather.55.cloned.1.call-start = ((), (), s32[]{:S(2)}) async-start(), calls=%async_computation.43 | async-start | bytes 3932160 | tf_op jit(solution)/shard_map/all_gather | solution.py:55
  1421.6 61.3 %all-reduce.81.cloned.1.call-start = ((), (), s32[]{:S(2)}) async-start(), calls=%async_computation.24 | async-start | bytes 131072 | tf_op jit(solution)/shard_map/psum | solution.py:46
  1456.8 80.0 %all-reduce.83.cloned.1.call-start = ((), (), s32[]{:S(2)}) async-start(), calls=%async_computation.25 | async-start | bytes 1572864 | tf_op jit(solution)/shard_map/psum | solution.py:54
  1509.0 55.9 %all-gather.57.cloned.1.call-start = ((), (), s32[]{:S(2)}) async-start(), calls=%async_computation.44 | async-start | bytes 3932160 | tf_op jit(solution)/shard_map/all_gather | solution.py:55
  1536.9 61.3 %all-reduce.85.cloned.1.call-start = ((), (), s32[]{:S(2)}) async-start(), calls=%async_computation.26 | async-start | bytes 131072 | tf_op jit(solution)/shard_map/psum | solution.py:46
  1572.1 81.4 %all-reduce.87.cloned.1.call-start = ((), (), s32[]{:S(2)}) async-start(), calls=%async_computation.27 | async-start | bytes 1572864 | tf_op jit(solution)/shard_map/psum | solution.py:54
  1625.9 84.9 %all-gather.59.cloned.1.call-start = ((), (), s32[]{:S(2)}) async-start(), calls=%async_computation.45 | async-start | bytes 3932160 | tf_op jit(solution)/shard_map/all_gather | solution.py:55
  1653.5 91.1 %all-reduce.89.cloned.1.call-start = ((), (), s32[]{:S(2)}) async-start(), calls=%async_computation.28 | async-start | bytes 131072 | tf_op jit(solution)/shard_map/psum | solution.py:46
  1717.5 82.9 %all-reduce.91.cloned.1.call-start = ((), (), s32[]{:S(2)}) async-start(), calls=%async_computation.29 | async-start | bytes 1572864 | tf_op jit(solution)/shard_map/psum | solution.py:54
  1772.5 84.5 %all-gather.61.cloned.1.call-start = ((), (), s32[]{:S(2)}) async-start(), calls=%async_computation.46 | async-start | bytes 3932160 | tf_op jit(solution)/shard_map/all_gather | solution.py:55
  1800.4 90.2 %all-reduce.93.cloned.1.call-start = ((), (), s32[]{:S(2)}) async-start(), calls=%async_computation.30 | async-start | bytes 131072 | tf_op jit(solution)/shard_map/psum | solution.py:46
  1863.4 82.3 %all-reduce.95.cloned.1.call-start = ((), (), s32[]{:S(2)}) async-start(), calls=%async_computation.31 | async-start | bytes 1572864 | tf_op jit(solution)/shard_map/psum | solution.py:54
  1918.1 85.1 %all-gather.63.cloned.1.call-start = ((), (), s32[]{:S(2)}) async-start(), calls=%async_computation.47 | async-start | bytes 3932160 | tf_op jit(solution)/shard_map/all_gather | solution.py:55
  (54 other events, 723.9 us)
Sparse Core Ops, SparseCore 0:
  15.4 26.8 all-reduce.32
  68.3 27.7 all-reduce.34
  97.6 26.5 all-gather.32
  140.4 25.9 all-reduce.36
  194.1 27.4 all-reduce.38
  223.0 26.5 all-gather.34
  264.6 25.9 all-reduce.40
  318.4 27.7 all-reduce.42
  347.7 26.5 all-gather.36
  389.4 25.8 all-reduce.44
  444.8 27.4 all-reduce.46
  473.6 26.5 all-gather.38
  511.4 25.9 all-reduce.48
  563.5 27.7 all-reduce.50
  592.6 26.5 all-gather.40
  630.4 25.8 all-reduce.52
  684.0 27.4 all-reduce.54
  712.9 26.5 all-gather.42
  751.7 25.8 all-reduce.56
  803.7 27.7 all-reduce.58
  833.0 26.5 all-gather.44
  871.8 25.8 all-reduce.60
  925.4 27.4 all-reduce.62
  954.3 26.5 all-gather.46
  989.9 25.8 all-reduce.64
  1042.0 27.7 all-reduce.66
  1071.1 26.5 all-gather.48
  1106.7 25.8 all-reduce.68
  1160.5 27.4 all-reduce.70
  1189.3 26.5 all-gather.50
  1224.2 25.8 all-reduce.72
  1276.3 27.7 all-reduce.74
  1305.5 26.5 all-gather.52
  1340.3 25.8 all-reduce.76
  1394.1 27.4 all-reduce.78
  1423.0 26.5 all-gather.54
  1457.0 25.9 all-reduce.80
  1509.1 27.7 all-reduce.82
  1538.2 26.5 all-gather.56
  1572.2 25.8 all-reduce.84
  1626.0 27.4 all-reduce.86
  1655.0 26.5 all-gather.58
  1717.6 26.9 all-reduce.88
  1772.6 27.7 all-reduce.90
  1801.7 26.5 all-gather.60
  1863.5 27.0 all-reduce.92
  1918.2 27.4 all-reduce.94
  1947.1 26.5 all-gather.62
where the time goes:
time: 2040 us; the launch traced here: 2030 us
  waiting for transfers between devices  1110 us (54%)
  other arithmetic  408 us (20%)
  matrix products  334 us (16%)
  local copies, waits for them, and re-layouts  153 us (8%)
    psum x16, waiting for transfers between devices, local_part(): diag_blk = lax.psum(jnp.where(my_row == owner_row, diag_local, 0.0), 'pr')  395 us
    psum x16, waiting for transfers between devices, local_part(): lax.psum(jnp.where(my_col == owner_col, below_diag.reshape(local_rows, bl...  392 us
    all_gather x16, waiting for transfers between devices, local_part(): gathered = lax.all_gather(row_panel, 'pr', axis=0, tiled=False)  319 us
    dot_general x16, matrix products, apply_update(): lax.dot_general(rows_part, trail_view, (((1,), (1,)), ((), ())), precisio...  215 us
    another operation x48, other arithmetic, local_part(): l_diag = jnp.linalg.cholesky(diag_blk)  199 us
    another operation x32, other arithmetic, solve_right(): lax.linalg.triangular_solve(l_diag, right_side, left_side=False, lower=Tr...  168 us
    dot_general x15, matrix products, apply_update(): jnp.einsum('rc,mbc->rmb', rows_part, col_view[col_start:panel_dev], preci...  71.8 us
    another operation x16, matrix products, solve_right(): lax.linalg.triangular_solve(l_diag, right_side, left_side=False, lower=Tr...  47.4 us
  transfers between devices with their start and end apart: 48, of which 45 were waited for; matrix products, arithmetic and copies ran while one was open for 14% of the time, Pallas kernels for 0%

commit v1 on v0

v1 whole, which is shorter than its diff:
```python
import jax
import jax.numpy as jnp
from jax import lax
from jax.experimental import pallas as pl
from jax.experimental.pallas import tpu as pltpu
from jax.sharding import PartitionSpec as P

HIGH = lax.Precision.HIGHEST
MESH = pl.DeviceIdType.MESH
NB = 128
PAIRS = 8


def dot_nt(a, b):
    return lax.dot_general(a, b, (((1,), (1,)), ((), ())), precision=HIGH, preferred_element_type=jnp.float32)


def dot_nn(a, b):
    return lax.dot_general(a, b, (((1,), (0,)), ((), ())), precision=HIGH, preferred_element_type=jnp.float32)


def lane_of(x, lane):
    return jnp.broadcast_to(x[:, lane:lane + 1], (8, NB))


def row_of(x, row):
    return jnp.broadcast_to(x[row:row + 1, :], (8, NB))


def factor_block(load, store_upper, store_inv):
    lane = lax.broadcasted_iota(jnp.int32, (8, NB), 1)
    sub = lax.broadcasted_iota(jnp.int32, (8, NB), 0)
    rows = [load(i) for i in range(16)]
    for g in range(16):
        base = 8 * g
        inside = (lane >= base) & (lane < base + 8)
        cols = [lane_of(rows[g], base + t) for t in range(8)]
        cur = jnp.where(inside, jnp.where(lane - base == sub, 1.0, 0.0), rows[g])
        recips, pivots, cross = [], [], {}
        for s in range(8):
            recip = 1.0 / row_of(cols[s], s)
            pivot = row_of(cur, s)
            mult = jnp.where(sub > s, cols[s] * recip, 0.0)
            for t in range(s + 1, 8):
                cross[t, s] = row_of(cols[t], s)
                cols[t] = cols[t] - mult * cross[t, s]
            if s < 7:
                cur = cur - mult * pivot
            recips.append(recip)
            pivots.append(pivot)
        for i in range(g + 1, 16):
            part = [lane_of(rows[i], base + t) for t in range(8)]
            acc = jnp.where(inside, 0.0, rows[i])
            for s in range(8):
                mult = part[s] * recips[s]
                for t in range(s + 1, 8):
                    part[t] = part[t] - mult * cross[t, s]
                acc = acc - mult * pivots[s]
            rows[i] = acc
        diag = cols[7]
        upper = jnp.where(lane > base + 7, cur, 0.0)
        for t in range(8):
            if t < 7:
                diag = jnp.where(sub == t, cols[t], diag)
            upper = jnp.where((lane == base + t) & (sub <= t), cols[t], upper)
        scale = lax.rsqrt(diag)
        scale = scale * (1.5 - 0.5 * diag * scale * scale)
        store_upper(g, upper * scale)
        store_inv(g, jnp.where(lane < base + 8, cur, 0.0) * scale)


def body(pan, lead, trail, pan_out, trail_out, work, cols, diag, upper, inv, tile, zero,
         lead_sem, own_sem, own_send, own_recv, keep_sem, give_send, give_recv, pass_send, far_send, far_recv,
         in_sem, out_sem, pan_sem):
    my_row = lax.axis_index("pr")
    my_col = lax.axis_index("pc")
    chip = my_row // 2
    core = my_row % 2
    across = {"pr": my_row, "pc": 1 - my_col}
    beside = {"pr": 2 * chip + 1 - core, "pc": my_col}
    along = {"pr": 2 * (1 - chip) + core, "pc": my_col}
    is_giver = core == my_col

    barrier = pltpu.get_barrier_semaphore()
    for peer in (across, beside, along):
        pl.semaphore_signal(barrier, inc=1, device_id=peer, device_id_type=MESH)

    def half(c):
        return pl.ds(pl.multiple_of(c * NB, NB), NB)

    for p in range(PAIRS):
        for c in range(2):
            for r in range(4):
                for q in range(4):
                    pltpu.make_async_copy(lead.at[q, c, p, r], work.at[p, 4 * r + q, :, pl.ds(c * NB, NB)], lead_sem.at[p]).start()
    for p in range(PAIRS):
        pltpu.make_async_copy(pan.at[p, 4:12], work.at[p, 16:24, :, half(my_col)], own_sem.at[p]).start()
    zero[...] = jnp.zeros_like(zero)
    pl.semaphore_wait(barrier, 3)

    def own_copy(p):
        return pltpu.make_async_remote_copy(
            src_ref=pan.at[p, 4:12], dst_ref=work.at[p, 16:24, :, half(my_col)],
            send_sem=own_send.at[p], recv_sem=own_recv.at[p], device_id=across, device_id_type=MESH)

    def own_arrival(p):
        return pltpu.make_async_remote_copy(
            src_ref=pan.at[p, 4:12], dst_ref=work.at[p, 16:24, :, half(1 - my_col)],
            send_sem=own_send.at[p], recv_sem=own_recv.at[p], device_id=across, device_id_type=MESH)

    for p in range(PAIRS):
        own_copy(p).start()

    def keep_copy(p):
        return pltpu.make_async_copy(work.at[p, 16:24], cols.at[p, :, chip], keep_sem.at[p])

    def give_copy(p):
        return pltpu.make_async_remote_copy(
            src_ref=work.at[p, 16:24], dst_ref=cols.at[p, :, chip],
            send_sem=give_send.at[p], recv_sem=give_recv.at[p], device_id=beside, device_id_type=MESH)

    def far_copy(p):
        return pltpu.make_async_remote_copy(
            src_ref=work.at[p, 16:24], dst_ref=cols.at[p, :, chip],
            send_sem=far_send.at[p], recv_sem=far_recv.at[p], device_id=along, device_id_type=MESH)

    def far_arrival(p):
        return pltpu.make_async_remote_copy(
            src_ref=work.at[p, 16:24], dst_ref=cols.at[p, :, 1 - chip],
            send_sem=far_send.at[p], recv_sem=far_recv.at[p], device_id=along, device_id_type=MESH)

    def pass_copy(p):
        return pltpu.make_async_remote_copy(
            src_ref=cols.at[p, :, 1 - chip], dst_ref=cols.at[p, :, 1 - chip],
            send_sem=pass_send.at[p], recv_sem=far_recv.at[p], device_id=beside, device_id_type=MESH)

    def rows256(p, c):
        return work[p, pl.ds(2 * c, 2)].reshape(256, 256)

    def set_rows256(p, c, value):
        work[p, pl.ds(2 * c, 2)] = value.reshape(2, NB, 256)

    def factor(h, p):
        def store_upper(g, value):
            upper[8 * g:8 * g + 8, :] = value

        def store_inv(g, value):
            inv[h * NB + 8 * g:h * NB + 8 * g + 8, h * NB:(h + 1) * NB] = value

        factor_block(lambda i: diag[8 * i:8 * i + 8, :], store_upper, store_inv)
        work[p, 2 * p + h, :, h * NB:(h + 1) * NB] = upper[...].T

    inv[0:NB, NB:256] = jnp.zeros((NB, NB), jnp.float32)

    def chain_step(p, carry):
        pltpu.make_async_copy(work.at[p, 0:16], work.at[p, 0:16], lead_sem.at[p]).wait()
        pltpu.make_async_copy(pan.at[p, 4:12], work.at[p, 16:24, :, half(my_col)], own_sem.at[p]).wait()
        own_arrival(p).wait_recv()

        def subtract(q, carry):
            right = rows256(q, p)

            def one(c, carry):
                set_rows256(p, c, rows256(p, c) - dot_nt(rows256(q, c), right))
                return carry

            return lax.fori_loop(p, 12, one, carry)

        lax.fori_loop(0, p, subtract, 0)

        diag[...] = work[p, 2 * p, :, 0:NB]
        factor(0, p)
        work[p, 2 * p, :, NB:256] = jnp.zeros((NB, NB), jnp.float32)
        inv0 = inv[0:NB, 0:NB]
        low = dot_nt(work[p, 2 * p + 1, :, 0:NB], inv0)
        work[p, 2 * p + 1, :, 0:NB] = low
        diag[...] = work[p, 2 * p + 1, :, NB:256] - dot_nt(low, low)
        factor(1, p)
        inv[NB:256, 0:NB] = -dot_nn(inv[NB:256, NB:256], dot_nn(low, inv0))

        def solve(c, carry):
            set_rows256(p, c, dot_nt(rows256(p, c), inv[...]))
            return carry

        lax.fori_loop(p + 1, 12, solve, 0)

        @pl.when(is_giver)
        def _():
            keep_copy(p).start()
            give_copy(p).start()
            far_copy(p).start()

            @pl.when(p > 0)
            def _():
                far_arrival(p - 1).wait_recv()
                pass_copy(p - 1).start()

        return carry

    lax.fori_loop(0, PAIRS, chain_step, 0)

    @pl.when(is_giver)
    def _():
        far_arrival(PAIRS - 1).wait_recv()
        pass_copy(PAIRS - 1).start()

    def pan_result(p, r):
        block = 4 * r + my_row
        return (pltpu.make_async_copy(work.at[p, block, :, half(my_col)], pan_out.at[p, r], pan_sem.at[0]),
                pltpu.make_async_copy(zero, pan_out.at[p, r], pan_sem.at[0]))

    def start_pan(p, carry):
        pltpu.make_async_copy(work.at[p, 16:24, :, half(my_col)], pan_out.at[p, 4:12], pan_sem.at[0]).start()
        for r in range(4):
            filled, empty = pan_result(p, r)
            below = 4 * r + my_row >= 2 * p + my_col

            @pl.when(below)
            def _():
                filled.start()

            @pl.when(jnp.logical_not(below))
            def _():
                empty.start()

        return carry

    lax.fori_loop(0, PAIRS, start_pan, 0)

    def tile_in(b, slot):
        return pltpu.make_async_copy(trail.at[pl.ds(512, 1024), pl.ds(pl.multiple_of(b * 256, 256), 256)],
                                     tile.at[slot, pl.ds(512, 1024)], in_sem.at[slot])

    def tile_out(b, slot):
        return pltpu.make_async_copy(tile.at[slot], trail_out.at[:, pl.ds(pl.multiple_of(b * 256, 256), 256)], out_sem.at[slot])

    tile_in(0, 0).start()

    def drain(p, carry):
        @pl.when(is_giver)
        def _():
            keep_copy(p).wait()

        @pl.when(jnp.logical_not(is_giver))
        def _():
            pltpu.make_async_remote_copy(
                src_ref=work.at[p, 16:24], dst_ref=cols.at[p, :, chip],
                send_sem=give_send.at[p], recv_sem=give_recv.at[p], device_id=beside, device_id_type=MESH).wait_recv()
            far_arrival(p).wait_recv()

        return carry

    lax.fori_loop(0, PAIRS, drain, 0)

    def trail_step(b, carry):
        slot = b % 2

        @pl.when(b > 0)
        def _():
            tile_out(b - 1, 1 - slot).wait()

        @pl.when(b < 7)
        def _():
            tile_in(b + 1, 1 - slot).start()

        for r in range(4):
            block = 4 * r + my_row
            p = block // 2
            side = half(block % 2)
            tile[slot, r * NB:(r + 1) * NB, :] = dot_nt(work[p, block, :, side], cols[p, b, :, :, side].reshape(256, NB))
        tile_in(b, slot).wait()

        def subtract(q, carry):
            right = cols[q, b].reshape(256, 256)

            def one(c, carry):
                where = pl.ds(512 + c * 256, 256)
                tile[slot, where, :] = tile[slot, where, :] - dot_nt(rows256(q, 8 + c), right)
                return carry

            return lax.fori_loop(0, 4, one, carry)

        lax.fori_loop(0, PAIRS, subtract, 0)
        tile_out(b, slot).start()
        return carry

    lax.fori_loop(0, 8, trail_step, 0)
    tile_out(7, 1).wait()
    pltpu.make_async_copy(pan_out, pan_out, pan_sem.at[0]).wait()

    def finish(p, carry):
        own_copy(p).wait_send()

        @pl.when(is_giver)
        def _():
            give_copy(p).wait_send()
            far_copy(p).wait_send()
            pass_copy(p).wait_send()

        return carry

    lax.fori_loop(0, PAIRS, finish, 0)


def solution(mesh):
    def local_part(panel_tile, trail_tile):
        pan = panel_tile.transpose(1, 0, 2).reshape(PAIRS, 12, NB, NB)
        lead = lax.all_gather(lax.all_gather(pan[:, 0:4], "pc", axis=0), "pr", axis=0)
        any_spec = pl.BlockSpec(memory_space=pl.ANY)
        dma = pltpu.SemaphoreType.DMA
        pan_out, trail_out = pl.pallas_call(
            body,
            out_shape=(jax.ShapeDtypeStruct(pan.shape, jnp.float32), jax.ShapeDtypeStruct(trail_tile.shape, jnp.float32)),
            in_specs=[any_spec] * 3,
            out_specs=(any_spec, any_spec),
            scratch_shapes=[
                pltpu.VMEM((PAIRS, 24, NB, 256), jnp.float32),
                pltpu.VMEM((PAIRS, 8, 2, NB, 256), jnp.float32),
                pltpu.VMEM((NB, NB), jnp.float32),
                pltpu.VMEM((NB, NB), jnp.float32),
                pltpu.VMEM((256, 256), jnp.float32),
                pltpu.VMEM((2, 1536, 256), jnp.float32),
                pltpu.VMEM((NB, NB), jnp.float32),
                dma((PAIRS,)), dma((PAIRS,)), dma((PAIRS,)), dma((PAIRS,)), dma((PAIRS,)), dma((PAIRS,)), dma((PAIRS,)),
                dma((PAIRS,)), dma((PAIRS,)), dma((PAIRS,)), dma((2,)), dma((2,)), dma((1,)),
            ],
            compiler_params=pltpu.CompilerParams(collective_id=0, has_side_effects=True, vmem_limit_bytes=64 * 1024 * 1024 - 65536),
            name="factor",
        )(pan, lead, trail_tile)
        return pan_out.reshape(PAIRS, 1536, NB).transpose(1, 0, 2), trail_out

    spec_panel = P("pr", "pc", None)
    spec_trail = P("pr", "pc")
    return jax.shard_map(local_part, mesh=mesh, in_specs=(spec_panel, spec_trail), out_specs=(spec_panel, spec_trail), check_vma=False)
```

time: 2040 us -> 540 us (0.26)
  waiting for transfers between devices: 1110 us -> 161 us
  other arithmetic: 408 us -> 0 us
  matrix products: 334 us -> 0 us
  Pallas kernels: 0 us -> 329 us
  local copies, waits for them, and re-layouts: 153 us -> 30.8 us
    psum x32 -> x0, waiting for transfers between devices: 788 us -> none  [the longest x16 395 us: local_part(): diag_blk = lax.psum(jnp.where(my_row == owner_row, diag_local, 0.0), 'pr')]
    another operation x80 -> x0, other arithmetic: 367 us -> none  [the longest x48 199 us: local_part(): l_diag = jnp.linalg.cholesky(diag_blk)]
    pallas_call x0 -> x1, Pallas kernels: none -> 329 us  [local_part(): pl.pallas_call(body, out_shape=(jax.ShapeDtypeStruct(pan.shape, jnp.float...]
    dot_general x31 -> x0, matrix products: 287 us -> none  [the longest x16 215 us: apply_update(): lax.dot_general(rows_part, trail_view, (((1,), (1,)), ((), ())), precisio...]
    all_gather x16 -> x2, waiting for transfers between devices: 319 us -> 161 us  [the longest x1 107 us: local_part(): lax.all_gather(lax.all_gather(pan[:, 0:4], 'pc', axis=0), 'pr', axis=0)]
    another operation x16 -> x0, matrix products: 47.4 us -> none  [solve_right(): lax.linalg.triangular_solve(l_diag, right_side, left_side=False, lower=Tr...]
    all_gather x16 -> x0, local copies, waits for them, and re-layouts: 37.8 us -> none  [local_part(): gathered = lax.all_gather(row_panel, 'pr', axis=0, tiled=False)]
    unnamed x110 -> x3, local copies, waits for them, and re-layouts: 46.2 us -> 14.2 us
  transfers between devices with their start and end apart: 48 -> 2, of which waited for: 45 -> 2; matrix products, arithmetic and copies ran while one was open for 14% -> 0% of each run, Pallas kernels for 0% -> 0%
where the time goes in v1:
time: 540 us; the launch traced here: 535 us
  Pallas kernels  329 us (61%)
  waiting for transfers between devices  161 us (30%)
  local copies, waits for them, and re-layouts  30.8 us (6%)
  between operations  14.1 us (3%)
    pallas_call x1, Pallas kernels, local_part(): pl.pallas_call(body, out_shape=(jax.ShapeDtypeStruct(pan.shape, jnp.float...  329 us
    all_gather x1, waiting for transfers between devices, local_part(): lax.all_gather(lax.all_gather(pan[:, 0:4], 'pc', axis=0), 'pr', axis=0)  107 us
    all_gather x1, waiting for transfers between devices, local_part(): lax.all_gather(pan[:, 0:4], 'pc', axis=0)  54.1 us
    unnamed x3, local copies, waits for them, and re-layouts  14.2 us
    reshape x1, local copies, waits for them, and re-layouts, local_part(): return (pan_out.reshape(PAIRS, 1536, NB).transpose(1, 0, 2), trail_out)  11.1 us
  transfers between devices with their start and end apart: 2, of which 2 were waited for; matrix products, arithmetic and copies ran while one was open for 0% of the time, Pallas kernels for 0%

profile of v1, /device:TPU:4, one launch (start us, length us, event | category | flops | bytes accessed | tf_op | source)
XLA Modules:
  0.0 535.1 jit_solution(3468718460562378618)
XLA Ops:
  7.2 0.0 all-gather.5.cloned.1.call-start
  7.2 4.0 copy.6
  11.2 0.0 copy-start
  11.2 2.7 copy-done
  13.9 1.5 slice.4
  15.4 0.0 all-gather.5.cloned.1.call-update
  15.4 0.0 all-gather.7.cloned.1.call-start
  15.5 54.1 %all-gather.5.cloned.1.call-done = f32[16,4,128,128]{3,2,1,0:T(8,128)} async-done(((f32[8,4,128,128]{3,2,1,0:T(8,128)}), f32[16,4,128,128]{3,2,1,0:T(8,128)}) %all-gather.5.cloned.1.call-update) | async-done | bytes 4194320 | tf_op jit(solution)/shard_map/all_gather | solution.py:308
  69.6 0.0 all-gather.7.cloned.1.call-update
  69.6 106.8 %all-gather.7.cloned.1.call-done = f32[8,8,4,128,128]{4,3,2,1,0:T(8,128)} async-done(((f32[2,8,4,128,128]{4,3,2,1,0:T(8,128)}), f32[8,8,4,128,128]{4,3,2,1,0:T(8,128)}) %all-gather.7.cloned.1.call-update) | async-done | bytes 16777232 | tf_op jit(solution)/shard_map/all_gather | solution.py:308
  176.4 329.3 %factor.1 = (f32[8,12,128,128]{3,2,1,0:T(8,128)}, f32[1536,2048]{1,0:T(8,128)}) custom-call(f32[8,12,128,128]{3,2,1,0:T(8,128)} %bitcast.9, f32[4,2,8,4,128,128]{5,4,3,2,1,0:T(8,128)} %bitcast.10, f32[1536,2048]{1,0:T(8,128)} %trail.1), custom_call_target="tpu_custom_call" | custom-call | tf_op jit(solution)/shard_map/factor/pallas_call | solution.py:311
  505.7 11.1 %copy.9 = f32[8,1536,128]{2,0,1:T(8,128)} copy(f32[8,1536,128]{2,1,0:T(8,128)} %bitcast.13) | data formatting | bytes 12582912 | tf_op jit(solution)/shard_map/reshape | solution.py:330
  516.7 11.5 %copy.11 = f32[1536,2048]{1,0:T(8,128)} copy(f32[1536,2048]{1,0:T(8,128)} %get-tuple-element.9) | data formatting | bytes 25165824
Async XLA Ops:
  7.2 62.4 %all-gather.5.cloned.1.call-start = ((), (), s32[]{:S(2)}) async-start(), calls=%async_computation | async-start | bytes 6291456 | tf_op jit(solution)/shard_map/all_gather | solution.py:308
  11.2 2.7 copy-start
  15.4 161.0 %all-gather.7.cloned.1.call-start = ((), (), s32[]{:S(2)}) async-start(), calls=%async_computation.1 | async-start | bytes 20971520 | tf_op jit(solution)/shard_map/all_gather | solution.py:308
Sparse Core Ops, SparseCore 0:
  15.5 53.9 all-gather.4
  71.1 105.2 all-gather.6

commit v2 on v1

v2 whole, which is shorter than its diff:
```python
import jax
import jax.numpy as jnp
from jax import lax
from jax.experimental import pallas as pl
from jax.experimental.pallas import tpu as pltpu
from jax.sharding import PartitionSpec as P

HIGH = lax.Precision.HIGHEST
MESH = pl.DeviceIdType.MESH
NB = 128
PAIRS = 8


def dot_nt(a, b):
    return lax.dot_general(a, b, (((1,), (1,)), ((), ())), precision=HIGH, preferred_element_type=jnp.float32)


def dot_nn(a, b):
    return lax.dot_general(a, b, (((1,), (0,)), ((), ())), precision=HIGH, preferred_element_type=jnp.float32)


def lane_of(x, lane):
    return jnp.broadcast_to(x[:, lane:lane + 1], (8, NB))


def row_of(x, row):
    return jnp.broadcast_to(x[row:row + 1, :], (8, NB))


def factor_block(load, store_upper, store_inv, beside=None):
    lane = lax.broadcasted_iota(jnp.int32, (8, NB), 1)
    sub = lax.broadcasted_iota(jnp.int32, (8, NB), 0)
    rows = [load(i) for i in range(16)]
    for g in range(16):
        base = 8 * g
        inside = (lane >= base) & (lane < base + 8)
        cols = [lane_of(rows[g], base + t) for t in range(8)]
        cur = jnp.where(inside, jnp.where(lane - base == sub, 1.0, 0.0), rows[g])
        recips, pivots, cross = [], [], {}
        for s in range(8):
            recip = 1.0 / row_of(cols[s], s)
            pivot = row_of(cur, s)
            mult = jnp.where(sub > s, cols[s] * recip, 0.0)
            for t in range(s + 1, 8):
                cross[t, s] = row_of(cols[t], s)
                cols[t] = cols[t] - mult * cross[t, s]
            if s < 7:
                cur = cur - mult * pivot
            recips.append(recip)
            pivots.append(pivot)
        for i in range(g + 1, 16):
            part = [lane_of(rows[i], base + t) for t in range(8)]
            acc = jnp.where(inside, 0.0, rows[i])
            for s in range(8):
                mult = part[s] * recips[s]
                for t in range(s + 1, 8):
                    part[t] = part[t] - mult * cross[t, s]
                acc = acc - mult * pivots[s]
            rows[i] = acc
        if beside is not None:
            beside(g)
        diag = cols[7]
        upper = jnp.where(lane > base + 7, cur, 0.0)
        for t in range(8):
            if t < 7:
                diag = jnp.where(sub == t, cols[t], diag)
            upper = jnp.where((lane == base + t) & (sub <= t), cols[t], upper)
        scale = lax.rsqrt(diag)
        scale = scale * (1.5 - 0.5 * diag * scale * scale)
        store_upper(g, upper * scale)
        store_inv(g, jnp.where(lane < base + 8, cur, 0.0) * scale)


def body(pan, trail, pan_out, trail_out, work, cols, schur, diag, upper, inv, gmat, top, zero,
         lead_sem, lead_send, lead_recv, own_sem, own_send, own_recv, keep_sem, give_send, give_recv, pass_send,
         far_send, far_recv, in_sem, out_sem, top_sem, pan_sem):
    my_row = lax.axis_index("pr")
    my_col = lax.axis_index("pc")
    chip = my_row // 2
    core = my_row % 2
    beside_row = 2 * chip + 1 - core
    along_row = 2 * (1 - chip) + core
    cross_row = 2 * (1 - chip) + 1 - core
    across = {"pr": my_row, "pc": 1 - my_col}
    beside = {"pr": beside_row, "pc": my_col}
    along = {"pr": along_row, "pc": my_col}
    is_giver = core == my_col

    barrier = pltpu.get_barrier_semaphore()
    for peer in (across, beside, along):
        pl.semaphore_signal(barrier, inc=1, device_id=peer, device_id_type=MESH)

    def half(c):
        return pl.ds(pl.multiple_of(c * NB, NB), NB)

    def remote(src, dst, send, recv, peer):
        return pltpu.make_async_remote_copy(src_ref=src, dst_ref=dst, send_sem=send, recv_sem=recv,
                                            device_id=peer, device_id_type=MESH)

    def strip(p, first, row, col):
        return work.at[p, first:4, row, :, half(col)]

    def mine(p, first):
        return pan.at[p, 0, first:4]

    def for_pair(p, fn):
        if isinstance(p, int):
            fn(p // 2)
        else:
            for first in range(4):
                pl.when(p // 2 == first)(lambda first=first: fn(first))

    def keep_strip(p, first):
        return pltpu.make_async_copy(mine(p, first), strip(p, first, my_row, my_col), lead_sem.at[p])

    def lead_copy(p, first, kind):
        out = strip(p, first, my_row, my_col)
        src, dst, peer = {
            0: (mine(p, first), out, beside),
            1: (mine(p, first), out, along),
            2: (mine(p, first), out, across),
            3: (strip(p, first, my_row, 1 - my_col), strip(p, first, my_row, 1 - my_col), along),
            4: (strip(p, first, along_row, my_col), strip(p, first, along_row, my_col), beside),
            5: (strip(p, first, my_row, 1 - my_col), strip(p, first, my_row, 1 - my_col), beside),
            6: (strip(p, first, along_row, 1 - my_col), strip(p, first, along_row, 1 - my_col), beside),
            7: (strip(p, first, along_row, my_col), strip(p, first, along_row, my_col), across),
        }[kind]
        slot = 3 if kind == 7 else kind
        return remote(src, dst, lead_send.at[p, slot], lead_recv.at[p, slot], peer)

    def lead_arrival(p, first, kind):
        row, col = [(beside_row, my_col), (along_row, my_col), (my_row, 1 - my_col), (along_row, 1 - my_col),
                    (cross_row, my_col), (beside_row, 1 - my_col), (cross_row, 1 - my_col)][kind]
        return remote(mine(p, first), strip(p, first, row, col), lead_send.at[p, kind], lead_recv.at[p, kind], beside)

    def stage_one(p):
        def go(first):
            for kind in (1, 2, 0):
                lead_copy(p, first, kind).start()

        for_pair(p, go)

    def stage_two(p):
        def go(first):
            lead_arrival(p, first, 1).wait_recv()
            lead_arrival(p, first, 2).wait_recv()

            @pl.when(core == 0)
            def _():
                lead_copy(p, first, 3).start()

            @pl.when(core == 1)
            def _():
                lead_copy(p, first, 7).start()

            lead_copy(p, first, 4).start()
            lead_copy(p, first, 5).start()

        for_pair(p, go)

    def stage_three(p):
        def go(first):
            lead_arrival(p, first, 3).wait_recv()
            lead_copy(p, first, 6).start()

        for_pair(p, go)

    def lead_wait(p):
        def go(first):
            keep_strip(p, first).wait()
            for kind in (0, 4, 5, 6):
                lead_arrival(p, first, kind).wait_recv()
            for kind in range(7):
                lead_copy(p, first, kind).wait_send()

        for_pair(p, go)

    def keep_own(p):
        return pltpu.make_async_copy(pan.at[p, 1:3], work.at[p, 4:6, :, :, half(my_col)], own_sem.at[p])

    def own_copy(p):
        return remote(pan.at[p, 1:3], work.at[p, 4:6, :, :, half(my_col)], own_send.at[p], own_recv.at[p], across)

    def own_arrival(p):
        return remote(pan.at[p, 1:3], work.at[p, 4:6, :, :, half(1 - my_col)], own_send.at[p], own_recv.at[p], across)

    def keep_copy(p):
        return pltpu.make_async_copy(work.at[p, 4:6], cols.at[p, :, :, chip], keep_sem.at[p])

    def give_copy(p):
        return remote(work.at[p, 4:6], cols.at[p, :, :, chip], give_send.at[p], give_recv.at[p], beside)

    def far_copy(p):
        return remote(work.at[p, 4:6], cols.at[p, :, :, chip], far_send.at[p], far_recv.at[p], along)

    def far_arrival(p):
        return remote(work.at[p, 4:6], cols.at[p, :, :, 1 - chip], far_send.at[p], far_recv.at[p], along)

    def pass_copy(p):
        return remote(cols.at[p, :, :, 1 - chip], cols.at[p, :, :, 1 - chip], pass_send.at[p], far_recv.at[p], beside)

    def cols_wait(p):
        @pl.when(is_giver)
        def _():
            keep_copy(p).wait()

        @pl.when(jnp.logical_not(is_giver))
        def _():
            give_copy(p).wait_recv()
            far_arrival(p).wait_recv()

    def rows256(p, c):
        return work[p, c // 2, pl.ds(2 * (c % 2), 2)].reshape(256, 256)

    def set_rows256(p, c, value):
        work[p, c // 2, pl.ds(2 * (c % 2), 2)] = value.reshape(2, NB, 256)

    def rows512(p, c):
        return work[p, c].reshape(512, 256)

    def set_rows512(p, c, value):
        work[p, c] = value.reshape(4, NB, 256)

    def tile_in(b):
        return pltpu.make_async_copy(trail.at[pl.ds(512, 1024), pl.ds(b * 256, 256)], schur.at[b], in_sem.at[b])

    for p in range(PAIRS):
        keep_strip(p, p // 2).start()
    zero[...] = jnp.zeros_like(zero)
    pl.semaphore_wait(barrier, 3)
    stage_one(0)
    for p in range(PAIRS):
        keep_own(p).start()
    for b in range(8):
        tile_in(b).start()
    stage_two(0)
    stage_one(1)
    own_copy(0).start()
    stage_three(0)

    def schur_update(q, b, c):
        where = pl.ds(c * 256, 256)
        right = cols[q, b // 4, b % 4].reshape(256, 256)
        schur[b, where, :] = schur[b, where, :] - dot_nt(rows256(q, 8 + c), right)

    def idle_or_update(p, h, g):
        idle = p < 2
        c = g % 4
        b = 4 * h + g // 4
        hi = jnp.where(idle, 0, 4 + c // 2)
        lo = jnp.where(idle, 0, 2 * (c % 2))
        left = work[jnp.where(idle, 0, p - 2), hi, pl.ds(lo, 2)].reshape(256, 256)
        right = cols[jnp.where(idle, PAIRS - 1, p - 2), h, g // 4].reshape(256, 256)
        b = jnp.where(idle, 8, b)
        where = pl.ds(c * 256, 256)
        schur[b, where, :] = schur[b, where, :] - dot_nt(left, right)

    def factor(h, p):
        def store_upper(g, value):
            upper[8 * g:8 * g + 8, :] = value

        def store_inv(g, value):
            inv[h, 8 * g:8 * g + 8, :] = value

        factor_block(lambda i: diag[8 * i:8 * i + 8, :], store_upper, store_inv, lambda g: idle_or_update(p, h, g))
        work[p, p // 2, 2 * (p % 2) + h, :, half(h)] = upper[...].T

    gmat[...] = jnp.zeros_like(gmat)

    def chain_step(p, carry):
        lead_wait(p)

        @pl.when(p + 2 < PAIRS)
        def _():
            stage_one(p + 2)

        @pl.when(p + 1 < PAIRS)
        def _():
            own_copy(p + 1).start()

        def subtract(q, carry):
            right = rows256(q, p)

            def one(c, carry):
                set_rows256(p, c, rows256(p, c) - dot_nt(rows256(q, c), right))
                return carry

            return lax.fori_loop(p, 8, one, carry)

        lax.fori_loop(0, p, subtract, 0)

        @pl.when(p == 2)
        def _():
            for b in range(8):
                tile_in(b).wait()

        @pl.when(p >= 2)
        def _():
            cols_wait(p - 2)

        hi, lo = p // 2, 2 * (p % 2)
        diag[...] = work[p, hi, lo, :, 0:NB]

        def factor_half(h, carry):
            factor(h, p)

            @pl.when(h == 0)
            def _():
                work[p, hi, lo, :, NB:256] = jnp.zeros((NB, NB), jnp.float32)
                low = dot_nt(work[p, hi, lo + 1, :, 0:NB], inv[0])
                work[p, hi, lo + 1, :, 0:NB] = low
                diag[...] = work[p, hi, lo + 1, :, NB:256] - dot_nt(low, low)

            @pl.when((h == 0) & (p + 1 < PAIRS))
            def _():
                stage_two(p + 1)

            return carry

        lax.fori_loop(0, 2, factor_half, 0)

        @pl.when(p + 1 < PAIRS)
        def _():
            stage_three(p + 1)

        @pl.when(is_giver & (p > 0))
        def _():
            far_arrival(p - 1).wait_recv()
            pass_copy(p - 1).start()

        gmat[0:NB, 0:NB] = inv[0]
        gmat[NB:256, NB:256] = inv[1]
        gmat[NB:256, 0:NB] = -dot_nn(inv[1], dot_nn(work[p, hi, lo + 1, :, 0:NB], inv[0]))

        keep_own(p).wait()
        own_arrival(p).wait_recv()

        def subtract_own(q, carry):
            right = rows256(q, p)

            def one(c, carry):
                set_rows512(p, c, rows512(p, c) - dot_nt(rows512(q, c), right))
                return carry

            return lax.fori_loop(4, 6, one, carry)

        lax.fori_loop(0, p, subtract_own, 0)

        def solve(c, carry):
            set_rows256(p, c, dot_nt(rows256(p, c), gmat[...]))
            return carry

        lax.fori_loop(p + 1, 12, solve, 0)

        @pl.when(is_giver)
        def _():
            far_copy(p).start()
            keep_copy(p).start()
            give_copy(p).start()

        return carry

    lax.fori_loop(0, PAIRS, chain_step, 0)

    def start_pan(p, carry):
        pltpu.make_async_copy(work.at[p, 4:6, :, :, half(my_col)], pan_out.at[p, 1:3], pan_sem.at[0]).start()
        for r in range(4):
            below = 4 * r + my_row >= 2 * p + my_col

            @pl.when(below)
            def _():
                pltpu.make_async_copy(work.at[p, r, my_row, :, half(my_col)], pan_out.at[p, 0, r], pan_sem.at[0]).start()

            @pl.when(jnp.logical_not(below))
            def _():
                pltpu.make_async_copy(zero, pan_out.at[p, 0, r], pan_sem.at[0]).start()

        return carry

    lax.fori_loop(0, PAIRS, start_pan, 0)

    def tail(q):
        cols_wait(q)

        def one(i, carry):
            schur_update(q, i // 4, i % 4)
            return carry

        lax.fori_loop(0, 32, one, 0)

    tail(PAIRS - 2)

    @pl.when(is_giver)
    def _():
        far_arrival(PAIRS - 1).wait_recv()
        pass_copy(PAIRS - 1).start()

    cols_wait(PAIRS - 1)

    def cols_of(b):
        return pl.ds(pl.multiple_of(b * 256, 256), 256)

    def schur_out(b):
        return pltpu.make_async_copy(schur.at[b], trail_out.at[pl.ds(512, 1024), cols_of(b)], out_sem.at[b])

    def top_out(b, slot):
        return pltpu.make_async_copy(top.at[slot], trail_out.at[pl.ds(0, 512), cols_of(b)], top_sem.at[slot])

    def last_step(b, carry):
        def one(c, carry):
            schur_update(PAIRS - 1, b, c)
            return carry

        lax.fori_loop(0, 4, one, 0)
        schur_out(b).start()
        slot = b % 2

        @pl.when(b >= 2)
        def _():
            top_out(b - 2, slot).wait()

        for r in range(4):
            p = 2 * r + my_row // 2
            side = half(my_row % 2)
            top[slot, r * NB:(r + 1) * NB, :] = dot_nt(work[p, r, my_row, :, side],
                                                       cols[p, b // 4, b % 4, :, :, side].reshape(256, NB))
        top_out(b, slot).start()
        return carry

    lax.fori_loop(0, 8, last_step, 0)
    top_out(6, 0).wait()
    top_out(7, 1).wait()
    for b in range(8):
        schur_out(b).wait()
    pltpu.make_async_copy(pan_out, pan_out, pan_sem.at[0]).wait()

    def finish(p, carry):
        own_copy(p).wait_send()

        @pl.when(is_giver)
        def _():
            give_copy(p).wait_send()
            far_copy(p).wait_send()
            pass_copy(p).wait_send()

        return carry

    lax.fori_loop(0, PAIRS, finish, 0)


def solution(mesh):
    def local_part(panel_tile, trail_tile):
        pan = panel_tile.transpose(1, 0, 2).reshape(PAIRS, 3, 4, NB, NB)
        any_spec = pl.BlockSpec(memory_space=pl.ANY)
        dma = pltpu.SemaphoreType.DMA
        pan_out, trail_out = pl.pallas_call(
            body,
            out_shape=(jax.ShapeDtypeStruct(pan.shape, jnp.float32), jax.ShapeDtypeStruct(trail_tile.shape, jnp.float32)),
            in_specs=[any_spec] * 2,
            out_specs=(any_spec, any_spec),
            scratch_shapes=[
                pltpu.VMEM((PAIRS, 6, 4, NB, 256), jnp.float32),
                pltpu.VMEM((PAIRS, 2, 4, 2, NB, 256), jnp.float32),
                pltpu.VMEM((9, 1024, 256), jnp.float32),
                pltpu.VMEM((NB, NB), jnp.float32),
                pltpu.VMEM((NB, NB), jnp.float32),
                pltpu.VMEM((2, NB, NB), jnp.float32),
                pltpu.VMEM((256, 256), jnp.float32),
                pltpu.VMEM((2, 512, 256), jnp.float32),
                pltpu.VMEM((NB, NB), jnp.float32),
                dma((PAIRS,)), dma((PAIRS, 7)), dma((PAIRS, 7)), dma((PAIRS,)), dma((PAIRS,)), dma((PAIRS,)), dma((PAIRS,)),
                dma((PAIRS,)), dma((PAIRS,)), dma((PAIRS,)), dma((PAIRS,)), dma((PAIRS,)), dma((8,)), dma((8,)), dma((2,)),
                dma((1,)),
            ],
            compiler_params=pltpu.CompilerParams(collective_id=0, has_side_effects=True, vmem_limit_bytes=64 * 1024 * 1024 - 65536),
            name="factor",
        )(pan, trail_tile)
        return pan_out.reshape(PAIRS, 1536, NB).transpose(1, 0, 2), trail_out

    spec_panel = P("pr", "pc", None)
    spec_trail = P("pr", "pc")
    return jax.shard_map(local_part, mesh=mesh, in_specs=(spec_panel, spec_trail), out_specs=(spec_panel, spec_trail), check_vma=False)
```

time: 540 us -> 292 us (0.54)
  waiting for transfers between devices: 161 us -> 0 us
  Pallas kernels: 329 us -> 262 us
  between operations: 14.1 us -> 0.64 us
    all_gather x2 -> x0, waiting for transfers between devices: 161 us -> none  [the longest x1 107 us: local_part(): lax.all_gather(lax.all_gather(pan[:, 0:4], 'pc', axis=0), 'pr', axis=0)]
    pallas_call x1, Pallas kernels: 329 us -> 262 us  [local_part(): pl.pallas_call(body, out_shape=(jax.ShapeDtypeStruct(pan.shape, jnp.float...]
    unnamed x3 -> x1, local copies, waits for them, and re-layouts: 14.2 us -> 11.5 us
  transfers between devices with their start and end apart: 2 -> 0, of which waited for: 2 -> 0; matrix products, arithmetic and copies ran while one was open for 0% -> 0% of each run, Pallas kernels for 0% -> 0%
where the time goes in v2:
time: 292 us
  Pallas kernels  262 us (90%)
  local copies, waits for them, and re-layouts  29.3 us (10%)
    pallas_call x1, Pallas kernels, local_part(): pl.pallas_call(body, out_shape=(jax.ShapeDtypeStruct(pan.shape, jnp.float...  262 us
    unnamed x1, local copies, waits for them, and re-layouts  11.5 us
    reshape x1, local copies, waits for them, and re-layouts, local_part(): return (pan_out.reshape(PAIRS, 1536, NB).transpose(1, 0, 2), trail_out)  11.1 us
    transpose x1, local copies, waits for them, and re-layouts, local_part(): pan = panel_tile.transpose(1, 0, 2).reshape(PAIRS, 3, 4, NB, NB)  6.7 us

profile of v2, /device:TPU:4, one launch (start us, length us, event | category | flops | bytes accessed | tf_op | source)
XLA Modules:
  0.0 292.0 jit_solution(13101784836093197129)
XLA Ops:
  0.6 6.7 %copy.4 = f32[8,1536,128]{2,1,0:T(8,128)} copy(f32[8,1536,128]{2,0,1:T(8,128)} %bitcast.7) | data formatting | bytes 12582912 | tf_op jit(solution)/shard_map/transpose | solution.py:453
  7.3 262.0 %factor.1 = (f32[8,3,4,128,128]{4,3,2,1,0:T(8,128)}, f32[1536,2048]{1,0:T(8,128)}) custom-call(f32[8,3,4,128,128]{4,3,2,1,0:T(8,128)} %bitcast.6, f32[1536,2048]{1,0:T(8,128)} %trail.1), custom_call_target="tpu_custom_call" | custom-call | tf_op jit(solution)/shard_map/factor/pallas_call | solution.py:456
  269.4 11.1 %copy.7 = f32[8,1536,128]{2,0,1:T(8,128)} copy(f32[8,1536,128]{2,1,0:T(8,128)} %bitcast.9) | data formatting | bytes 12582912 | tf_op jit(solution)/shard_map/reshape | solution.py:478
  280.4 11.5 %copy.9 = f32[1536,2048]{1,0:T(8,128)} copy(f32[1536,2048]{1,0:T(8,128)} %get-tuple-element.9) | data formatting | bytes 25165824

commit v3 on v2

--- a/solution.py
+++ b/solution.py
@@ -71,9 +71,9 @@
         store_inv(g, jnp.where(lane < base + 8, cur, 0.0) * scale)
 
 
-def body(pan, trail, pan_out, trail_out, work, cols, schur, diag, upper, inv, gmat, top, zero,
+def body(pan, trail, pan_out, schur_out, top_out, left_out, right_out, work, cols, schur, diag, upper, inv, gmat, top, zero,
          lead_sem, lead_send, lead_recv, own_sem, own_send, own_recv, keep_sem, give_send, give_recv, pass_send,
-         far_send, far_recv, in_sem, out_sem, top_sem, pan_sem):
+         far_send, far_recv, in_sem, out_sem, top_sem, left_sem, pan_sem):
     my_row = lax.axis_index("pr")
     my_col = lax.axis_index("pc")
     chip = my_row // 2
@@ -215,11 +215,11 @@
     def set_rows256(p, c, value):
         work[p, c // 2, pl.ds(2 * (c % 2), 2)] = value.reshape(2, NB, 256)
 
-    def rows512(p, c):
-        return work[p, c].reshape(512, 256)
-
-    def set_rows512(p, c, value):
-        work[p, c] = value.reshape(4, NB, 256)
+    def own_rows(p):
+        return work[p, 4:6].reshape(1024, 256)
+
+    def set_own(p, value):
+        work[p, 4:6] = value.reshape(2, 4, NB, 256)
 
     def tile_in(b):
         return pltpu.make_async_copy(trail.at[pl.ds(512, 1024), pl.ds(b * 256, 256)], schur.at[b], in_sem.at[b])
@@ -243,18 +243,6 @@
         right = cols[q, b // 4, b % 4].reshape(256, 256)
         schur[b, where, :] = schur[b, where, :] - dot_nt(rows256(q, 8 + c), right)
 
-    def idle_or_update(p, h, g):
-        idle = p < 2
-        c = g % 4
-        b = 4 * h + g // 4
-        hi = jnp.where(idle, 0, 4 + c // 2)
-        lo = jnp.where(idle, 0, 2 * (c % 2))
-        left = work[jnp.where(idle, 0, p - 2), hi, pl.ds(lo, 2)].reshape(256, 256)
-        right = cols[jnp.where(idle, PAIRS - 1, p - 2), h, g // 4].reshape(256, 256)
-        b = jnp.where(idle, 8, b)
-        where = pl.ds(c * 256, 256)
-        schur[b, where, :] = schur[b, where, :] - dot_nt(left, right)
-
     def factor(h, p):
         def store_upper(g, value):
             upper[8 * g:8 * g + 8, :] = value
@@ -262,7 +250,17 @@
         def store_inv(g, value):
             inv[h, 8 * g:8 * g + 8, :] = value
 
-        factor_block(lambda i: diag[8 * i:8 * i + 8, :], store_upper, store_inv, lambda g: idle_or_update(p, h, g))
+        def load(i):
+            return diag[8 * i:8 * i + 8, :]
+
+        @pl.when(p < 2)
+        def _():
+            factor_block(load, store_upper, store_inv)
+
+        @pl.when(p >= 2)
+        def _():
+            factor_block(load, store_upper, store_inv, lambda g: schur_update(p - 2, 4 * h + g // 4, g % 4))
+
         work[p, p // 2, 2 * (p % 2) + h, :, half(h)] = upper[...].T
 
     gmat[...] = jnp.zeros_like(gmat)
@@ -336,13 +334,8 @@
         own_arrival(p).wait_recv()
 
         def subtract_own(q, carry):
-            right = rows256(q, p)
-
-            def one(c, carry):
-                set_rows512(p, c, rows512(p, c) - dot_nt(rows512(q, c), right))
-                return carry
-
-            return lax.fori_loop(4, 6, one, carry)
+            set_own(p, own_rows(p) - dot_nt(own_rows(q), rows256(q, p)))
+            return carry
 
         lax.fori_loop(0, p, subtract_own, 0)
 
@@ -350,7 +343,8 @@
             set_rows256(p, c, dot_nt(rows256(p, c), gmat[...]))
             return carry
 
-        lax.fori_loop(p + 1, 12, solve, 0)
+        lax.fori_loop(p + 1, 8, solve, 0)
+        set_own(p, dot_nt(own_rows(p), gmat[...]))
 
         @pl.when(is_giver)
         def _():
@@ -379,16 +373,32 @@
 
     lax.fori_loop(0, PAIRS, start_pan, 0)
 
-    def tail(q):
-        cols_wait(q)
-
-        def one(i, carry):
-            schur_update(q, i // 4, i % 4)
+    cols_wait(PAIRS - 2)
+
+    def left_copy():
+        return pltpu.make_async_copy(work.at[PAIRS - 1, 4:6], left_out, left_sem.at[0])
+
+    def right_copy():
+        return pltpu.make_async_copy(cols.at[PAIRS - 1], right_out, left_sem.at[1])
+
+    def schur_copy(b):
+        return pltpu.make_async_copy(schur.at[b], schur_out.at[b], out_sem.at[b])
+
+    def top_copy(b, slot):
+        return pltpu.make_async_copy(top.at[slot], top_out.at[b], top_sem.at[slot])
+
+    left_copy().start()
+
+    def tail(b, carry):
+        def one(c, carry):
+            schur_update(PAIRS - 2, b, c)
             return carry
 
-        lax.fori_loop(0, 32, one, 0)
-
-    tail(PAIRS - 2)
+        lax.fori_loop(0, 4, one, 0)
+        schur_copy(b).start()
+        return carry
+
+    lax.fori_loop(0, 8, tail, 0)
 
     @pl.when(is_giver)
     def _():
@@ -396,42 +406,30 @@
         pass_copy(PAIRS - 1).start()
 
     cols_wait(PAIRS - 1)
-
-    def cols_of(b):
-        return pl.ds(pl.multiple_of(b * 256, 256), 256)
-
-    def schur_out(b):
-        return pltpu.make_async_copy(schur.at[b], trail_out.at[pl.ds(512, 1024), cols_of(b)], out_sem.at[b])
-
-    def top_out(b, slot):
-        return pltpu.make_async_copy(top.at[slot], trail_out.at[pl.ds(0, 512), cols_of(b)], top_sem.at[slot])
-
-    def last_step(b, carry):
-        def one(c, carry):
-            schur_update(PAIRS - 1, b, c)
-            return carry
-
-        lax.fori_loop(0, 4, one, 0)
-        schur_out(b).start()
+    right_copy().start()
+
+    def top_step(b, carry):
         slot = b % 2
 
         @pl.when(b >= 2)
         def _():
-            top_out(b - 2, slot).wait()
+            top_copy(b - 2, slot).wait()
 
         for r in range(4):
             p = 2 * r + my_row // 2
             side = half(my_row % 2)
             top[slot, r * NB:(r + 1) * NB, :] = dot_nt(work[p, r, my_row, :, side],
                                                        cols[p, b // 4, b % 4, :, :, side].reshape(256, NB))
-        top_out(b, slot).start()
+        top_copy(b, slot).start()
         return carry
 
-    lax.fori_loop(0, 8, last_step, 0)
-    top_out(6, 0).wait()
-    top_out(7, 1).wait()
+    lax.fori_loop(0, 8, top_step, 0)
+    top_copy(6, 0).wait()
+    top_copy(7, 1).wait()
     for b in range(8):
-        schur_out(b).wait()
+        schur_copy(b).wait()
+    left_copy().wait()
+    right_copy().wait()
     pltpu.make_async_copy(pan_out, pan_out, pan_sem.at[0]).wait()
 
     def finish(p, carry):
@@ -446,6 +444,18 @@
         return carry
 
     lax.fori_loop(0, PAIRS, finish, 0)
+
+
+def finish_body(schur, top, left, right, pan, trail_out, pan_out):
+    trail_out[0:512, :] = top[0]
+    right_tile = right[0, 0].reshape(256, 256)
+    for c in range(4):
+        where = slice(256 * c, 256 * c + 256)
+        rows = left[c // 2, 2 * (c % 2):2 * (c % 2) + 2].reshape(256, 256)
+        trail_out[512 + 256 * c:768 + 256 * c, :] = schur[0, where, :] - dot_nt(rows, right_tile)
+    flat = pan_out.reshape(192 * PAIRS, NB)
+    for p in range(PAIRS):
+        flat[pl.ds(p, 192, stride=PAIRS), :] = pan[p]
 
 
 def solution(mesh):
@@ -453,15 +463,18 @@
         pan = panel_tile.transpose(1, 0, 2).reshape(PAIRS, 3, 4, NB, NB)
         any_spec = pl.BlockSpec(memory_space=pl.ANY)
         dma = pltpu.SemaphoreType.DMA
-        pan_out, trail_out = pl.pallas_call(
+        f32 = jnp.float32
+        pan_out, schur, top, left, right = pl.pallas_call(
             body,
-            out_shape=(jax.ShapeDtypeStruct(pan.shape, jnp.float32), jax.ShapeDtypeStruct(trail_tile.shape, jnp.float32)),
+            out_shape=(jax.ShapeDtypeStruct(pan.shape, f32), jax.ShapeDtypeStruct((8, 1024, 256), f32),
+                       jax.ShapeDtypeStruct((8, 512, 256), f32), jax.ShapeDtypeStruct((2, 4, NB, 256), f32),
+                       jax.ShapeDtypeStruct((2, 4, 2, NB, 256), f32)),
             in_specs=[any_spec] * 2,
-            out_specs=(any_spec, any_spec),
+            out_specs=(any_spec,) * 5,
             scratch_shapes=[
                 pltpu.VMEM((PAIRS, 6, 4, NB, 256), jnp.float32),
                 pltpu.VMEM((PAIRS, 2, 4, 2, NB, 256), jnp.float32),
-                pltpu.VMEM((9, 1024, 256), jnp.float32),
+                pltpu.VMEM((8, 1024, 256), jnp.float32),
                 pltpu.VMEM((NB, NB), jnp.float32),
                 pltpu.VMEM((NB, NB), jnp.float32),
                 pltpu.VMEM((2, NB, NB), jnp.float32),
@@ -469,13 +482,28 @@
                 pltpu.VMEM((2, 512, 256), jnp.float32),
                 pltpu.VMEM((NB, NB), jnp.float32),
                 dma((PAIRS,)), dma((PAIRS, 7)), dma((PAIRS, 7)), dma((PAIRS,)), dma((PAIRS,)), dma((PAIRS,)), dma((PAIRS,)),
-                dma((PAIRS,)), dma((PAIRS,)), dma((PAIRS,)), dma((PAIRS,)), dma((PAIRS,)), dma((8,)), dma((8,)), dma((2,)),
+                dma((PAIRS,)), dma((PAIRS,)), dma((PAIRS,)), dma((PAIRS,)), dma((PAIRS,)), dma((8,)), dma((8,)), dma((2,)), dma((2,)),
                 dma((1,)),
             ],
             compiler_params=pltpu.CompilerParams(collective_id=0, has_side_effects=True, vmem_limit_bytes=64 * 1024 * 1024 - 65536),
             name="factor",
         )(pan, trail_tile)
-        return pan_out.reshape(PAIRS, 1536, NB).transpose(1, 0, 2), trail_out
+        trail_out, panel_out = pl.pallas_call(
+            finish_body,
+            grid=(8,),
+            out_shape=(jax.ShapeDtypeStruct(trail_tile.shape, f32), jax.ShapeDtypeStruct(panel_tile.shape, f32)),
+            in_specs=[
+                pl.BlockSpec((1, 1024, 256), lambda b: (b, 0, 0)),
+                pl.BlockSpec((1, 512, 256), lambda b: (b, 0, 0)),
+                pl.BlockSpec((2, 4, NB, 256), lambda b: (0, 0, 0, 0)),
+                pl.BlockSpec((1, 1, 2, NB, 256), lambda b: (b // 4, b % 4, 0, 0, 0)),
+                pl.BlockSpec((PAIRS, 192, NB), lambda b: (0, b, 0)),
+            ],
+            out_specs=(pl.BlockSpec((1536, 256), lambda b: (0, b)), pl.BlockSpec((192, PAIRS, NB), lambda b: (b, 0, 0))),
+            compiler_params=pltpu.CompilerParams(vmem_limit_bytes=48 * 1024 * 1024),
+            name="finish",
+        )(schur, top, left, right, pan_out.reshape(PAIRS, 1536, NB))
+        return panel_out, trail_out
 
     spec_panel = P("pr", "pc", None)
     spec_trail = P("pr", "pc")

time: 292 us -> 269 us (0.921)
  local copies, waits for them, and re-layouts: 29.3 us -> 9.51 us
  Pallas kernels: 262 us -> 259 us
    reshape x1 -> x0, local copies, waits for them, and re-layouts: 11.1 us -> none  [local_part(): return (pan_out.reshape(PAIRS, 1536, NB).transpose(1, 0, 2), trail_out)]
    unnamed x1 -> x4, local copies, waits for them, and re-layouts: 11.5 us -> 2.81 us
    pallas_call x1 -> x2, Pallas kernels: 262 us -> 259 us  [the longest x1 240 us: local_part(): pl.pallas_call(body, out_shape=(jax.ShapeDtypeStruct(pan.shape, f32), jax...]
where the time goes in v3:
time: 269 us
  Pallas kernels  259 us (96%)
  local copies, waits for them, and re-layouts  9.51 us (4%)
    pallas_call x1, Pallas kernels, local_part(): pl.pallas_call(body, out_shape=(jax.ShapeDtypeStruct(pan.shape, f32), jax...  240 us
    pallas_call x1, Pallas kernels, local_part(): pl.pallas_call(finish_body, grid=(8,), out_shape=(jax.ShapeDtypeStruct(tr...  18.8 us
    transpose x1, local copies, waits for them, and re-layouts, local_part(): pan = panel_tile.transpose(1, 0, 2).reshape(PAIRS, 3, 4, NB, NB)  6.7 us

profile of v3, /device:TPU:4, one launch (start us, length us, event | category | flops | bytes accessed | tf_op | source)
XLA Modules:
  0.0 268.7 jit_solution(11233727302237297858)
XLA Ops:
  0.6 6.7 %copy.4 = f32[8,1536,128]{2,1,0:T(8,128)} copy(f32[8,1536,128]{2,0,1:T(8,128)} %bitcast.4) | data formatting | bytes 12582912 | tf_op jit(solution)/shard_map/transpose | solution.py:463
  7.3 239.8 %factor.1 = (f32[8,3,4,128,128]{4,3,2,1,0:T(8,128)}, f32[8,1024,256]{2,1,0:T(8,128)}, f32[8,512,256]{2,1,0:T(8,128)}, f32[2,4,128,256]{3,2,1,0:T(8,128)}, f32[2,4,2,128,256]{4,3,2,1,0:T(8,128)}) custom-call(f32[8,3,4,128,128]{4,3,2,1,0:T(8,128)} %bitcast.3, f32[1536,2048]{1,0:T(8,128)} %trail.1), custom_call_target="tpu_custom_call" | custom-call | tf_op jit(solution)/shard_map/factor/pallas_call | solution.py:467
  247.2 0.0 copy-start
  247.2 1.6 copy-done
  248.8 0.0 copy-start.1
  248.8 1.2 copy-done.1
  250.0 18.8 %finish.1 = (f32[1536,2048]{1,0:T(8,128)}, f32[1536,8,128]{2,1,0:T(8,128)}) custom-call(f32[8,1024,256]{2,1,0:T(8,128)} %get-tuple-element.9.schur, f32[8,512,256]{2,1,0:T(8,128)} %get-tuple-element.10.top, f32[2,4,128,256]{3,2,1,0:T(8,128)S(1)} %copy-done.1, f32[2,4,2,128,256]{4,3,2,1,0:T(8,128)S(1)} %copy-done, f32[8,1536,128]{2,1,0:T(8,128)} %bitcast.5), custom_call_target="tpu_custom_call" | custom-call | tf_op jit(solution)/shard_map/finish/pallas_call | solution.py:491
Async XLA Ops:
  247.2 1.6 copy-start
  248.8 1.2 copy-start.1

commit v4 on v3

--- a/solution.py
+++ b/solution.py
@@ -9,6 +9,8 @@
 MESH = pl.DeviceIdType.MESH
 NB = 128
 PAIRS = 8
+LAG = 3
+LAST = 2
 
 
 def dot_nt(a, b):
@@ -97,83 +99,75 @@
         return pltpu.make_async_remote_copy(src_ref=src, dst_ref=dst, send_sem=send, recv_sem=recv,
                                             device_id=peer, device_id_type=MESH)
 
-    def strip(p, first, row, col):
-        return work.at[p, first:4, row, :, half(col)]
-
-    def mine(p, first):
-        return pan.at[p, 0, first:4]
+    first_part = (0, 0, 1, 0)
+    second_part = (0, 1, 4, 1)
 
     def for_pair(p, fn):
         if isinstance(p, int):
-            fn(p // 2)
+            fn((p, p // 2, 4, p + 1))
         else:
             for first in range(4):
-                pl.when(p // 2 == first)(lambda first=first: fn(first))
-
-    def keep_strip(p, first):
-        return pltpu.make_async_copy(mine(p, first), strip(p, first, my_row, my_col), lead_sem.at[p])
-
-    def lead_copy(p, first, kind):
-        out = strip(p, first, my_row, my_col)
-        src, dst, peer = {
-            0: (mine(p, first), out, beside),
-            1: (mine(p, first), out, along),
-            2: (mine(p, first), out, across),
-            3: (strip(p, first, my_row, 1 - my_col), strip(p, first, my_row, 1 - my_col), along),
-            4: (strip(p, first, along_row, my_col), strip(p, first, along_row, my_col), beside),
-            5: (strip(p, first, my_row, 1 - my_col), strip(p, first, my_row, 1 - my_col), beside),
-            6: (strip(p, first, along_row, 1 - my_col), strip(p, first, along_row, 1 - my_col), beside),
-            7: (strip(p, first, along_row, my_col), strip(p, first, along_row, my_col), across),
+                pl.when(p // 2 == first)(lambda first=first: fn((p, first, 4, p + 1)))
+
+    def strip(part, row, col):
+        p, lo, hi, _ = part
+        return work.at[p, lo:hi, row, :, half(col)]
+
+    def mine(part):
+        p, lo, hi, _ = part
+        return pan.at[p, 0, lo:hi]
+
+    def keep_strip(part):
+        return pltpu.make_async_copy(mine(part), strip(part, my_row, my_col), lead_sem.at[part[3]])
+
+    def lead_copy(part, kind):
+        row, col, peer, slot = {
+            0: (my_row, my_col, beside, 0),
+            1: (my_row, my_col, along, 1),
+            2: (my_row, my_col, across, 2),
+            3: (my_row, 1 - my_col, along, 3),
+            4: (along_row, my_col, beside, 4),
+            5: (my_row, 1 - my_col, beside, 5),
+            6: (along_row, 1 - my_col, beside, 6),
+            7: (along_row, my_col, across, 3),
         }[kind]
-        slot = 3 if kind == 7 else kind
-        return remote(src, dst, lead_send.at[p, slot], lead_recv.at[p, slot], peer)
-
-    def lead_arrival(p, first, kind):
+        there = strip(part, row, col)
+        return remote(mine(part) if kind < 3 else there, there, lead_send.at[part[3], slot], lead_recv.at[part[3], slot], peer)
+
+    def lead_arrival(part, kind):
         row, col = [(beside_row, my_col), (along_row, my_col), (my_row, 1 - my_col), (along_row, 1 - my_col),
                     (cross_row, my_col), (beside_row, 1 - my_col), (cross_row, 1 - my_col)][kind]
-        return remote(mine(p, first), strip(p, first, row, col), lead_send.at[p, kind], lead_recv.at[p, kind], beside)
-
-    def stage_one(p):
-        def go(first):
-            for kind in (1, 2, 0):
-                lead_copy(p, first, kind).start()
-
-        for_pair(p, go)
-
-    def stage_two(p):
-        def go(first):
-            lead_arrival(p, first, 1).wait_recv()
-            lead_arrival(p, first, 2).wait_recv()
-
-            @pl.when(core == 0)
-            def _():
-                lead_copy(p, first, 3).start()
-
-            @pl.when(core == 1)
-            def _():
-                lead_copy(p, first, 7).start()
-
-            lead_copy(p, first, 4).start()
-            lead_copy(p, first, 5).start()
-
-        for_pair(p, go)
-
-    def stage_three(p):
-        def go(first):
-            lead_arrival(p, first, 3).wait_recv()
-            lead_copy(p, first, 6).start()
-
-        for_pair(p, go)
-
-    def lead_wait(p):
-        def go(first):
-            keep_strip(p, first).wait()
-            for kind in (0, 4, 5, 6):
-                lead_arrival(p, first, kind).wait_recv()
-            for kind in range(7):
-                lead_copy(p, first, kind).wait_send()
-
-        for_pair(p, go)
+        return remote(mine(part), strip(part, row, col), lead_send.at[part[3], kind], lead_recv.at[part[3], kind], beside)
+
+    def stage_one(part):
+        for kind in (1, 2, 0):
+            lead_copy(part, kind).start()
+
+    def stage_two(part):
+        lead_arrival(part, 1).wait_recv()
+        lead_arrival(part, 2).wait_recv()
+
+        @pl.when(core == 0)
+        def _():
+            lead_copy(part, 3).start()
+
+        @pl.when(core == 1)
+        def _():
+            lead_copy(part, 7).start()
+
+        lead_copy(part, 4).start()
+        lead_copy(part, 5).start()
+
+    def stage_three(part):
+        lead_arrival(part, 3).wait_recv()
+        lead_copy(part, 6).start()
+
+    def lead_wait(part):
+        keep_strip(part).wait()
+        for kind in (0, 4, 5, 6):
+            lead_arrival(part, kind).wait_recv()
+        for kind in range(7):
+            lead_copy(part, kind).wait_send()
 
     def keep_own(p):
         return pltpu.make_async_copy(pan.at[p, 1:3], work.at[p, 4:6, :, :, half(my_col)], own_sem.at[p])
@@ -224,19 +218,23 @@
     def tile_in(b):
         return pltpu.make_async_copy(trail.at[pl.ds(512, 1024), pl.ds(b * 256, 256)], schur.at[b], in_sem.at[b])
 
-    for p in range(PAIRS):
-        keep_strip(p, p // 2).start()
+    keep_strip(first_part).start()
+    keep_strip(second_part).start()
+    for p in range(1, PAIRS):
+        for_pair(p, lambda part: keep_strip(part).start())
     zero[...] = jnp.zeros_like(zero)
+    gmat[...] = jnp.zeros_like(gmat)
     pl.semaphore_wait(barrier, 3)
-    stage_one(0)
+    stage_one(first_part)
+    stage_two(first_part)
+    stage_one(second_part)
+    for_pair(1, stage_one)
+    stage_three(first_part)
     for p in range(PAIRS):
         keep_own(p).start()
     for b in range(8):
         tile_in(b).start()
-    stage_two(0)
-    stage_one(1)
-    own_copy(0).start()
-    stage_three(0)
+    lead_wait(first_part)
 
     def schur_update(q, b, c):
         where = pl.ds(c * 256, 256)
@@ -253,28 +251,20 @@
         def load(i):
             return diag[8 * i:8 * i + 8, :]
 
-        @pl.when(p < 2)
+        @pl.when(p < LAG)
         def _():
             factor_block(load, store_upper, store_inv)
 
-        @pl.when(p >= 2)
-        def _():
-            factor_block(load, store_upper, store_inv, lambda g: schur_update(p - 2, 4 * h + g // 4, g % 4))
+        @pl.when(p >= LAG)
+        def _():
+            factor_block(load, store_upper, store_inv, lambda g: schur_update(p - LAG, 4 * h + g // 4, g % 4))
 
         work[p, p // 2, 2 * (p % 2) + h, :, half(h)] = upper[...].T
 
-    gmat[...] = jnp.zeros_like(gmat)
-
-    def chain_step(p, carry):
-        lead_wait(p)
-
-        @pl.when(p + 2 < PAIRS)
-        def _():
-            stage_one(p + 2)
-
-        @pl.when(p + 1 < PAIRS)
-        def _():
-            own_copy(p + 1).start()
+    def lead_step(p):
+        @pl.when(p > 0)
+        def _():
+            for_pair(p, lead_wait)
 
         def subtract(q, carry):
             right = rows256(q, p)
@@ -287,14 +277,14 @@
 
         lax.fori_loop(0, p, subtract, 0)
 
-        @pl.when(p == 2)
+        @pl.when(p == LAG)
         def _():
             for b in range(8):
                 tile_in(b).wait()
 
-        @pl.when(p >= 2)
-        def _():
-            cols_wait(p - 2)
+        @pl.when(p >= LAG)
+        def _():
+            cols_wait(p - LAG)
 
         hi, lo = p // 2, 2 * (p % 2)
         diag[...] = work[p, hi, lo, :, 0:NB]
@@ -309,42 +299,65 @@
                 work[p, hi, lo + 1, :, 0:NB] = low
                 diag[...] = work[p, hi, lo + 1, :, NB:256] - dot_nt(low, low)
 
-            @pl.when((h == 0) & (p + 1 < PAIRS))
-            def _():
-                stage_two(p + 1)
+            @pl.when((h == 0) & (p == 0))
+            def _():
+                stage_two(second_part)
+                for_pair(2, stage_one)
+                for_pair(1, stage_two)
+
+            @pl.when((h == 0) & (p > 0) & (p + 1 < PAIRS))
+            def _():
+                for_pair(p + 1, stage_two)
+
+            @pl.when((h == 0) & (p + 3 < PAIRS))
+            def _():
+                for_pair(p + 3, stage_one)
+
+            @pl.when(h == 0)
+            def _():
+                own_copy(p).start()
 
             return carry
 
         lax.fori_loop(0, 2, factor_half, 0)
 
+        @pl.when(p == 0)
+        def _():
+            stage_three(second_part)
+
         @pl.when(p + 1 < PAIRS)
         def _():
-            stage_three(p + 1)
-
+            for_pair(p + 1, stage_three)
+
+        gmat[p % 2, 0:NB, 0:NB] = inv[0]
+        gmat[p % 2, NB:256, NB:256] = inv[1]
+        gmat[p % 2, NB:256, 0:NB] = -dot_nn(inv[1], dot_nn(work[p, hi, lo + 1, :, 0:NB], inv[0]))
+
+        @pl.when(p == 0)
+        def _():
+            lead_wait(second_part)
+
+        def solve(c, carry):
+            set_rows256(p, c, dot_nt(rows256(p, c), gmat[p % 2]))
+            return carry
+
+        lax.fori_loop(p + 1, 8, solve, 0)
+
+    def own_step(p):
         @pl.when(is_giver & (p > 0))
         def _():
             far_arrival(p - 1).wait_recv()
             pass_copy(p - 1).start()
 
-        gmat[0:NB, 0:NB] = inv[0]
-        gmat[NB:256, NB:256] = inv[1]
-        gmat[NB:256, 0:NB] = -dot_nn(inv[1], dot_nn(work[p, hi, lo + 1, :, 0:NB], inv[0]))
-
         keep_own(p).wait()
         own_arrival(p).wait_recv()
 
-        def subtract_own(q, carry):
+        def subtract(q, carry):
             set_own(p, own_rows(p) - dot_nt(own_rows(q), rows256(q, p)))
             return carry
 
-        lax.fori_loop(0, p, subtract_own, 0)
-
-        def solve(c, carry):
-            set_rows256(p, c, dot_nt(rows256(p, c), gmat[...]))
-            return carry
-
-        lax.fori_loop(p + 1, 8, solve, 0)
-        set_own(p, dot_nt(own_rows(p), gmat[...]))
+        lax.fori_loop(0, p, subtract, 0)
+        set_own(p, dot_nt(own_rows(p), gmat[p % 2]))
 
         @pl.when(is_giver)
         def _():
@@ -352,9 +365,18 @@
             keep_copy(p).start()
             give_copy(p).start()
 
+    def chain_step(p, carry):
+        @pl.when(p < PAIRS)
+        def _():
+            lead_step(p)
+
+        @pl.when(p > 0)
+        def _():
+            own_step(p - 1)
+
         return carry
 
-    lax.fori_loop(0, PAIRS, chain_step, 0)
+    lax.fori_loop(0, PAIRS + 1, chain_step, 0)
 
     def start_pan(p, carry):
         pltpu.make_async_copy(work.at[p, 4:6, :, :, half(my_col)], pan_out.at[p, 1:3], pan_sem.at[0]).start()
@@ -373,13 +395,11 @@
 
     lax.fori_loop(0, PAIRS, start_pan, 0)
 
-    cols_wait(PAIRS - 2)
-
     def left_copy():
-        return pltpu.make_async_copy(work.at[PAIRS - 1, 4:6], left_out, left_sem.at[0])
+        return pltpu.make_async_copy(work.at[PAIRS - LAST:PAIRS, 4:6], left_out, left_sem.at[0])
 
     def right_copy():
-        return pltpu.make_async_copy(cols.at[PAIRS - 1], right_out, left_sem.at[1])
+        return pltpu.make_async_copy(cols.at[PAIRS - LAST:PAIRS], right_out, left_sem.at[1])
 
     def schur_copy(b):
         return pltpu.make_async_copy(schur.at[b], schur_out.at[b], out_sem.at[b])
@@ -389,12 +409,16 @@
 
     left_copy().start()
 
+    for q in range(PAIRS - LAG, PAIRS - LAST):
+        cols_wait(q)
+
     def tail(b, carry):
-        def one(c, carry):
-            schur_update(PAIRS - 2, b, c)
-            return carry
-
-        lax.fori_loop(0, 4, one, 0)
+        for q in range(PAIRS - LAG, PAIRS - LAST):
+            def one(c, carry, q=q):
+                schur_update(q, b, c)
+                return carry
+
+            lax.fori_loop(0, 4, one, 0)
         schur_copy(b).start()
         return carry
 
@@ -405,7 +429,8 @@
         far_arrival(PAIRS - 1).wait_recv()
         pass_copy(PAIRS - 1).start()
 
-    cols_wait(PAIRS - 1)
+    for q in range(PAIRS - LAST, PAIRS):
+        cols_wait(q)
     right_copy().start()
 
     def top_step(b, carry):
@@ -448,11 +473,13 @@
 
 def finish_body(schur, top, left, right, pan, trail_out, pan_out):
     trail_out[0:512, :] = top[0]
-    right_tile = right[0, 0].reshape(256, 256)
     for c in range(4):
         where = slice(256 * c, 256 * c + 256)
-        rows = left[c // 2, 2 * (c % 2):2 * (c % 2) + 2].reshape(256, 256)
-        trail_out[512 + 256 * c:768 + 256 * c, :] = schur[0, where, :] - dot_nt(rows, right_tile)
+        total = schur[0, where, :]
+        for q in range(LAST):
+            rows = left[q, c // 2, 2 * (c % 2):2 * (c % 2) + 2].reshape(256, 256)
+            total = total - dot_nt(rows, right[q, 0, 0].reshape(256, 256))
+        trail_out[512 + 256 * c:768 + 256 * c, :] = total
     flat = pan_out.reshape(192 * PAIRS, NB)
     for p in range(PAIRS):
         flat[pl.ds(p, 192, stride=PAIRS), :] = pan[p]
@@ -467,8 +494,8 @@
         pan_out, schur, top, left, right = pl.pallas_call(
             body,
             out_shape=(jax.ShapeDtypeStruct(pan.shape, f32), jax.ShapeDtypeStruct((8, 1024, 256), f32),
-                       jax.ShapeDtypeStruct((8, 512, 256), f32), jax.ShapeDtypeStruct((2, 4, NB, 256), f32),
-                       jax.ShapeDtypeStruct((2, 4, 2, NB, 256), f32)),
+                       jax.ShapeDtypeStruct((8, 512, 256), f32), jax.ShapeDtypeStruct((LAST, 2, 4, NB, 256), f32),
+                       jax.ShapeDtypeStruct((LAST, 2, 4, 2, NB, 256), f32)),
             in_specs=[any_spec] * 2,
             out_specs=(any_spec,) * 5,
             scratch_shapes=[
@@ -478,10 +505,10 @@
                 pltpu.VMEM((NB, NB), jnp.float32),
                 pltpu.VMEM((NB, NB), jnp.float32),
                 pltpu.VMEM((2, NB, NB), jnp.float32),
-                pltpu.VMEM((256, 256), jnp.float32),
+                pltpu.VMEM((2, 256, 256), jnp.float32),
                 pltpu.VMEM((2, 512, 256), jnp.float32),
                 pltpu.VMEM((NB, NB), jnp.float32),
-                dma((PAIRS,)), dma((PAIRS, 7)), dma((PAIRS, 7)), dma((PAIRS,)), dma((PAIRS,)), dma((PAIRS,)), dma((PAIRS,)),
+                dma((PAIRS + 1,)), dma((PAIRS + 1, 7)), dma((PAIRS + 1, 7)), dma((PAIRS,)), dma((PAIRS,)), dma((PAIRS,)), dma((PAIRS,)),
                 dma((PAIRS,)), dma((PAIRS,)), dma((PAIRS,)), dma((PAIRS,)), dma((PAIRS,)), dma((8,)), dma((8,)), dma((2,)), dma((2,)),
                 dma((1,)),
             ],
@@ -495,12 +522,12 @@
             in_specs=[
                 pl.BlockSpec((1, 1024, 256), lambda b: (b, 0, 0)),
                 pl.BlockSpec((1, 512, 256), lambda b: (b, 0, 0)),
-                pl.BlockSpec((2, 4, NB, 256), lambda b: (0, 0, 0, 0)),
-                pl.BlockSpec((1, 1, 2, NB, 256), lambda b: (b // 4, b % 4, 0, 0, 0)),
+                pl.BlockSpec((LAST, 2, 4, NB, 256), lambda b: (0, 0, 0, 0, 0)),
+                pl.BlockSpec((LAST, 1, 1, 2, NB, 256), lambda b: (0, b // 4, b % 4, 0, 0, 0)),
                 pl.BlockSpec((PAIRS, 192, NB), lambda b: (0, b, 0)),
             ],
             out_specs=(pl.BlockSpec((1536, 256), lambda b: (0, b)), pl.BlockSpec((192, PAIRS, NB), lambda b: (b, 0, 0))),
-            compiler_params=pltpu.CompilerParams(vmem_limit_bytes=48 * 1024 * 1024),
+            compiler_params=pltpu.CompilerParams(vmem_limit_bytes=64 * 1024 * 1024 - 65536),
             name="finish",
         )(schur, top, left, right, pan_out.reshape(PAIRS, 1536, NB))
         return panel_out, trail_out

time: 269 us -> 265 us (0.985)
  local copies, waits for them, and re-layouts: 9.51 us -> 6.7 us
    pallas_call x1, Pallas kernels: 240 us -> 234 us  [local_part(): pl.pallas_call(body, out_shape=(jax.ShapeDtypeStruct(pan.shape, f32), jax...]
    pallas_call x1, Pallas kernels: 18.8 us -> 23.4 us  [local_part(): pl.pallas_call(finish_body, grid=(8,), out_shape=(jax.ShapeDtypeStruct(tr...]
    unnamed x4 -> x0, local copies, waits for them, and re-layouts: 2.81 us -> none
where the time goes in v4:
time: 265 us
  Pallas kernels  257 us (97%)
  local copies, waits for them, and re-layouts  6.7 us (3%)
    pallas_call x1, Pallas kernels, local_part(): pl.pallas_call(body, out_shape=(jax.ShapeDtypeStruct(pan.shape, f32), jax...  234 us
    pallas_call x1, Pallas kernels, local_part(): pl.pallas_call(finish_body, grid=(8,), out_shape=(jax.ShapeDtypeStruct(tr...  23.4 us
    transpose x1, local copies, waits for them, and re-layouts, local_part(): pan = panel_tile.transpose(1, 0, 2).reshape(PAIRS, 3, 4, NB, NB)  6.7 us

profile of v4, /device:TPU:4, one launch (start us, length us, event | category | flops | bytes accessed | tf_op | source)
XLA Modules:
  0.0 264.7 jit_solution(1340985874610859213)
XLA Ops:
  0.6 6.7 %copy.4 = f32[8,1536,128]{2,1,0:T(8,128)} copy(f32[8,1536,128]{2,0,1:T(8,128)} %bitcast.4) | data formatting | bytes 12582912 | tf_op jit(solution)/shard_map/transpose | solution.py:490
  7.3 233.9 %factor.1 = (f32[8,3,4,128,128]{4,3,2,1,0:T(8,128)}, f32[8,1024,256]{2,1,0:T(8,128)}, f32[8,512,256]{2,1,0:T(8,128)}, f32[2,2,4,128,256]{4,3,2,1,0:T(8,128)}, f32[2,2,4,2,128,256]{5,4,3,2,1,0:T(8,128)}) custom-call(f32[8,3,4,128,128]{4,3,2,1,0:T(8,128)} %bitcast.3, f32[1536,2048]{1,0:T(8,128)} %trail.1), custom_call_target="tpu_custom_call" | custom-call | tf_op jit(solution)/shard_map/factor/pallas_call | solution.py:494
  241.3 23.4 %finish.1 = (f32[1536,2048]{1,0:T(8,128)}, f32[1536,8,128]{2,1,0:T(8,128)}) custom-call(f32[8,1024,256]{2,1,0:T(8,128)} %get-tuple-element.9.schur, f32[8,512,256]{2,1,0:T(8,128)} %get-tuple-element.10.top, f32[2,2,4,128,256]{4,3,2,1,0:T(8,128)} %get-tuple-element.11.left, f32[2,2,4,2,128,256]{5,4,3,2,1,0:T(8,128)} %get-tuple-element.12.right, ...), custom_call_target="tpu_custom_call" | custom-call | tf_op jit(solution)/shard_map/finish/pallas_call | solution.py:518

commit v5 on v4

--- a/solution.py
+++ b/solution.py
@@ -209,6 +209,12 @@
     def set_rows256(p, c, value):
         work[p, c // 2, pl.ds(2 * (c % 2), 2)] = value.reshape(2, NB, 256)
 
+    def rows512(p, r):
+        return work[p, r].reshape(512, 256)
+
+    def set_rows512(p, r, value):
+        work[p, r] = value.reshape(4, NB, 256)
+
     def own_rows(p):
         return work[p, 4:6].reshape(1024, 256)
 
@@ -236,10 +242,8 @@
         tile_in(b).start()
     lead_wait(first_part)
 
-    def schur_update(q, b, c):
-        where = pl.ds(c * 256, 256)
-        right = cols[q, b // 4, b % 4].reshape(256, 256)
-        schur[b, where, :] = schur[b, where, :] - dot_nt(rows256(q, 8 + c), right)
+    def schur_update(q, b):
+        schur[b] = schur[b] - dot_nt(own_rows(q), cols[q, b // 4, b % 4].reshape(256, 256))
 
     def factor(h, p):
         def store_upper(g, value):
@@ -257,7 +261,11 @@
 
         @pl.when(p >= LAG)
         def _():
-            factor_block(load, store_upper, store_inv, lambda g: schur_update(p - LAG, 4 * h + g // 4, g % 4))
+            def beside(g):
+                if g % 4 == 0:
+                    schur_update(p - LAG, 4 * h + g // 4)
+
+            factor_block(load, store_upper, store_inv, beside)
 
         work[p, p // 2, 2 * (p % 2) + h, :, half(h)] = upper[...].T
 
@@ -269,11 +277,11 @@
         def subtract(q, carry):
             right = rows256(q, p)
 
-            def one(c, carry):
-                set_rows256(p, c, rows256(p, c) - dot_nt(rows256(q, c), right))
+            def one(r, carry):
+                set_rows512(p, r, rows512(p, r) - dot_nt(rows512(q, r), right))
                 return carry
 
-            return lax.fori_loop(p, 8, one, carry)
+            return lax.fori_loop(p // 2, 4, one, carry)
 
         lax.fori_loop(0, p, subtract, 0)
 
@@ -337,11 +345,15 @@
         def _():
             lead_wait(second_part)
 
-        def solve(c, carry):
-            set_rows256(p, c, dot_nt(rows256(p, c), gmat[p % 2]))
+        @pl.when(p % 2 == 0)
+        def _():
+            set_rows256(p, p + 1, dot_nt(rows256(p, p + 1), gmat[p % 2]))
+
+        def solve(r, carry):
+            set_rows512(p, r, dot_nt(rows512(p, r), gmat[p % 2]))
             return carry
 
-        lax.fori_loop(p + 1, 8, solve, 0)
+        lax.fori_loop(p // 2 + 1, 4, solve, 0)
 
     def own_step(p):
         @pl.when(is_giver & (p > 0))
@@ -414,11 +426,7 @@
 
     def tail(b, carry):
         for q in range(PAIRS - LAG, PAIRS - LAST):
-            def one(c, carry, q=q):
-                schur_update(q, b, c)
-                return carry
-
-            lax.fori_loop(0, 4, one, 0)
+            schur_update(q, b)
         schur_copy(b).start()
         return carry
 
@@ -473,13 +481,10 @@
 
 def finish_body(schur, top, left, right, pan, trail_out, pan_out):
     trail_out[0:512, :] = top[0]
-    for c in range(4):
-        where = slice(256 * c, 256 * c + 256)
-        total = schur[0, where, :]
-        for q in range(LAST):
-            rows = left[q, c // 2, 2 * (c % 2):2 * (c % 2) + 2].reshape(256, 256)
-            total = total - dot_nt(rows, right[q, 0, 0].reshape(256, 256))
-        trail_out[512 + 256 * c:768 + 256 * c, :] = total
+    total = schur[0]
+    for q in range(LAST):
+        total = total - dot_nt(left[q].reshape(1024, 256), right[q, 0, 0].reshape(256, 256))
+    trail_out[512:1536, :] = total
     flat = pan_out.reshape(192 * PAIRS, NB)
     for p in range(PAIRS):
         flat[pl.ds(p, 192, stride=PAIRS), :] = pan[p]

time: 265 us -> 257 us (0.970)
  the two profiles are of different devices: /device:TPU:4 before, /device:TPU:1 now
where the time goes in v5:
time: 257 us; the launch traced here: 256 us
  Pallas kernels  249 us (97%)
  local copies, waits for them, and re-layouts  6.7 us (3%)
    pallas_call x1, Pallas kernels, local_part(): pl.pallas_call(body, out_shape=(jax.ShapeDtypeStruct(pan.shape, f32), jax...  226 us
    pallas_call x1, Pallas kernels, local_part(): pl.pallas_call(finish_body, grid=(8,), out_shape=(jax.ShapeDtypeStruct(tr...  22.7 us
    transpose x1, local copies, waits for them, and re-layouts, local_part(): pan = panel_tile.transpose(1, 0, 2).reshape(PAIRS, 3, 4, NB, NB)  6.7 us

profile of v5, /device:TPU:1, one launch (start us, length us, event | category | flops | bytes accessed | tf_op | source)
XLA Modules:
  0.0 256.4 jit_solution(8216047805045883973)
XLA Ops:
  0.6 6.7 %copy.4 = f32[8,1536,128]{2,1,0:T(8,128)} copy(f32[8,1536,128]{2,0,1:T(8,128)} %bitcast.4) | data formatting | bytes 12582912 | tf_op jit(solution)/shard_map/transpose | solution.py:495
  7.3 226.3 %factor.1 = (f32[8,3,4,128,128]{4,3,2,1,0:T(8,128)}, f32[8,1024,256]{2,1,0:T(8,128)}, f32[8,512,256]{2,1,0:T(8,128)}, f32[2,2,4,128,256]{4,3,2,1,0:T(8,128)}, f32[2,2,4,2,128,256]{5,4,3,2,1,0:T(8,128)}) custom-call(f32[8,3,4,128,128]{4,3,2,1,0:T(8,128)} %bitcast.3, f32[1536,2048]{1,0:T(8,128)} %trail.1), custom_call_target="tpu_custom_call" | custom-call | tf_op jit(solution)/shard_map/factor/pallas_call | solution.py:499
  233.7 22.7 %finish.1 = (f32[1536,2048]{1,0:T(8,128)}, f32[1536,8,128]{2,1,0:T(8,128)}) custom-call(f32[8,1024,256]{2,1,0:T(8,128)} %get-tuple-element.9.schur, f32[8,512,256]{2,1,0:T(8,128)} %get-tuple-element.10.top, f32[2,2,4,128,256]{4,3,2,1,0:T(8,128)} %get-tuple-element.11.left, f32[2,2,4,2,128,256]{5,4,3,2,1,0:T(8,128)} %get-tuple-element.12.right, ...), custom_call_target="tpu_custom_call" | custom-call | tf_op jit(solution)/shard_map/finish/pallas_call | solution.py:523

commit v6 on v5

--- a/solution.py
+++ b/solution.py
@@ -36,7 +36,7 @@
     for g in range(16):
         base = 8 * g
         inside = (lane >= base) & (lane < base + 8)
-        cols = [lane_of(rows[g], base + t) for t in range(8)]
+        cols = [jnp.where(sub < 8, lane_of(rows[g], base + t), 0.0) for t in range(8)]
         cur = jnp.where(inside, jnp.where(lane - base == sub, 1.0, 0.0), rows[g])
         recips, pivots, cross = [], [], {}
         for s in range(8):
@@ -416,8 +416,21 @@
     def schur_copy(b):
         return pltpu.make_async_copy(schur.at[b], schur_out.at[b], out_sem.at[b])
 
-    def top_copy(b, slot):
-        return pltpu.make_async_copy(top.at[slot], top_out.at[b], top_sem.at[slot])
+    def top_copy(r):
+        return pltpu.make_async_copy(top.at[r % 2], top_out.at[r], top_sem.at[r % 2])
+
+    def top_rows(r):
+        if r >= 2:
+            top_copy(r - 2).wait()
+        p = 2 * r + my_row // 2
+        side = half(my_row % 2)
+
+        def one(b, carry):
+            top[r % 2, b] = dot_nt(work[p, r, my_row, :, side], cols[p, b // 4, b % 4, :, :, side].reshape(256, NB))
+            return carry
+
+        lax.fori_loop(0, 8, one, 0)
+        top_copy(r).start()
 
     left_copy().start()
 
@@ -432,6 +445,9 @@
 
     lax.fori_loop(0, 8, tail, 0)
 
+    for r in range(3):
+        top_rows(r)
+
     @pl.when(is_giver)
     def _():
         far_arrival(PAIRS - 1).wait_recv()
@@ -440,25 +456,9 @@
     for q in range(PAIRS - LAST, PAIRS):
         cols_wait(q)
     right_copy().start()
-
-    def top_step(b, carry):
-        slot = b % 2
-
-        @pl.when(b >= 2)
-        def _():
-            top_copy(b - 2, slot).wait()
-
-        for r in range(4):
-            p = 2 * r + my_row // 2
-            side = half(my_row % 2)
-            top[slot, r * NB:(r + 1) * NB, :] = dot_nt(work[p, r, my_row, :, side],
-                                                       cols[p, b // 4, b % 4, :, :, side].reshape(256, NB))
-        top_copy(b, slot).start()
-        return carry
-
-    lax.fori_loop(0, 8, top_step, 0)
-    top_copy(6, 0).wait()
-    top_copy(7, 1).wait()
+    top_rows(3)
+    top_copy(2).wait()
+    top_copy(3).wait()
     for b in range(8):
         schur_copy(b).wait()
     left_copy().wait()
@@ -480,7 +480,7 @@
 
 
 def finish_body(schur, top, left, right, pan, trail_out, pan_out):
-    trail_out[0:512, :] = top[0]
+    trail_out[0:512, :] = top[...].reshape(512, 256)
     total = schur[0]
     for q in range(LAST):
         total = total - dot_nt(left[q].reshape(1024, 256), right[q, 0, 0].reshape(256, 256))
@@ -499,7 +499,7 @@
         pan_out, schur, top, left, right = pl.pallas_call(
             body,
             out_shape=(jax.ShapeDtypeStruct(pan.shape, f32), jax.ShapeDtypeStruct((8, 1024, 256), f32),
-                       jax.ShapeDtypeStruct((8, 512, 256), f32), jax.ShapeDtypeStruct((LAST, 2, 4, NB, 256), f32),
+                       jax.ShapeDtypeStruct((4, 8, NB, 256), f32), jax.ShapeDtypeStruct((LAST, 2, 4, NB, 256), f32),
                        jax.ShapeDtypeStruct((LAST, 2, 4, 2, NB, 256), f32)),
             in_specs=[any_spec] * 2,
             out_specs=(any_spec,) * 5,
@@ -511,7 +511,7 @@
                 pltpu.VMEM((NB, NB), jnp.float32),
                 pltpu.VMEM((2, NB, NB), jnp.float32),
                 pltpu.VMEM((2, 256, 256), jnp.float32),
-                pltpu.VMEM((2, 512, 256), jnp.float32),
+                pltpu.VMEM((2, 8, NB, 256), jnp.float32),
                 pltpu.VMEM((NB, NB), jnp.float32),
                 dma((PAIRS + 1,)), dma((PAIRS + 1, 7)), dma((PAIRS + 1, 7)), dma((PAIRS,)), dma((PAIRS,)), dma((PAIRS,)), dma((PAIRS,)),
                 dma((PAIRS,)), dma((PAIRS,)), dma((PAIRS,)), dma((PAIRS,)), dma((PAIRS,)), dma((8,)), dma((8,)), dma((2,)), dma((2,)),
@@ -526,7 +526,7 @@
             out_shape=(jax.ShapeDtypeStruct(trail_tile.shape, f32), jax.ShapeDtypeStruct(panel_tile.shape, f32)),
             in_specs=[
                 pl.BlockSpec((1, 1024, 256), lambda b: (b, 0, 0)),
-                pl.BlockSpec((1, 512, 256), lambda b: (b, 0, 0)),
+                pl.BlockSpec((4, 1, NB, 256), lambda b: (0, b, 0, 0)),
                 pl.BlockSpec((LAST, 2, 4, NB, 256), lambda b: (0, 0, 0, 0, 0)),
                 pl.BlockSpec((LAST, 1, 1, 2, NB, 256), lambda b: (0, b // 4, b % 4, 0, 0, 0)),
                 pl.BlockSpec((PAIRS, 192, NB), lambda b: (0, b, 0)),

time: 257 us -> 252 us (0.981)
  Pallas kernels: 249 us -> 245 us
    pallas_call x1, Pallas kernels: 226 us -> 222 us  [local_part(): pl.pallas_call(body, out_shape=(jax.ShapeDtypeStruct(pan.shape, f32), jax...]
where the time goes in v6:
time: 252 us
  Pallas kernels  245 us (97%)
  local copies, waits for them, and re-layouts  6.7 us (3%)
    pallas_call x1, Pallas kernels, local_part(): pl.pallas_call(body, out_shape=(jax.ShapeDtypeStruct(pan.shape, f32), jax...  222 us
    pallas_call x1, Pallas kernels, local_part(): pl.pallas_call(finish_body, grid=(8,), out_shape=(jax.ShapeDtypeStruct(tr...  22.7 us
    transpose x1, local copies, waits for them, and re-layouts, local_part(): pan = panel_tile.transpose(1, 0, 2).reshape(PAIRS, 3, 4, NB, NB)  6.7 us

profile of v6, /device:TPU:1, one launch (start us, length us, event | category | flops | bytes accessed | tf_op | source)
XLA Modules:
  0.0 252.0 jit_solution(1523862821019665041)
XLA Ops:
  0.6 6.7 %copy.4 = f32[8,1536,128]{2,1,0:T(8,128)} copy(f32[8,1536,128]{2,0,1:T(8,128)} %bitcast.4) | data formatting | bytes 12582912 | tf_op jit(solution)/shard_map/transpose | solution.py:495
  7.3 221.9 %factor.1 = (f32[8,3,4,128,128]{4,3,2,1,0:T(8,128)}, f32[8,1024,256]{2,1,0:T(8,128)}, f32[4,8,128,256]{3,2,1,0:T(8,128)}, f32[2,2,4,128,256]{4,3,2,1,0:T(8,128)}, f32[2,2,4,2,128,256]{5,4,3,2,1,0:T(8,128)}) custom-call(f32[8,3,4,128,128]{4,3,2,1,0:T(8,128)} %bitcast.3, f32[1536,2048]{1,0:T(8,128)} %trail.1), custom_call_target="tpu_custom_call" | custom-call | tf_op jit(solution)/shard_map/factor/pallas_call | solution.py:499
  229.2 22.7 %finish.1 = (f32[1536,2048]{1,0:T(8,128)}, f32[1536,8,128]{2,1,0:T(8,128)}) custom-call(f32[8,1024,256]{2,1,0:T(8,128)} %get-tuple-element.9.schur, f32[4,8,128,256]{3,2,1,0:T(8,128)} %get-tuple-element.10.top, f32[2,2,4,128,256]{4,3,2,1,0:T(8,128)} %get-tuple-element.11.left, f32[2,2,4,2,128,256]{5,4,3,2,1,0:T(8,128)} %get-tuple-element.12.right, ...), custom_call_target="tpu_custom_call" | custom-call | tf_op jit(solution)/shard_map/finish/pallas_call | solution.py:523

commit v7 on v6

--- a/solution.py
+++ b/solution.py
@@ -236,10 +236,6 @@
     stage_one(second_part)
     for_pair(1, stage_one)
     stage_three(first_part)
-    for p in range(PAIRS):
-        keep_own(p).start()
-    for b in range(8):
-        tile_in(b).start()
     lead_wait(first_part)
 
     def schur_update(q, b):
@@ -310,20 +306,22 @@
             @pl.when((h == 0) & (p == 0))
             def _():
                 stage_two(second_part)
+                for_pair(1, stage_two)
                 for_pair(2, stage_one)
-                for_pair(1, stage_two)
+                for_pair(3, stage_one)
 
             @pl.when((h == 0) & (p > 0) & (p + 1 < PAIRS))
             def _():
-                for_pair(p + 1, stage_two)
-
-            @pl.when((h == 0) & (p + 3 < PAIRS))
-            def _():
-                for_pair(p + 3, stage_one)
+                for_pair(p + 1, stage_three)
 
             @pl.when(h == 0)
             def _():
-                own_copy(p).start()
+                keep_own(p).start()
+
+            @pl.when((h == 0) & (p == 1))
+            def _():
+                for b in range(8):
+                    tile_in(b).start()
 
             return carry
 
@@ -332,10 +330,6 @@
         @pl.when(p == 0)
         def _():
             stage_three(second_part)
-
-        @pl.when(p + 1 < PAIRS)
-        def _():
-            for_pair(p + 1, stage_three)
 
         gmat[p % 2, 0:NB, 0:NB] = inv[0]
         gmat[p % 2, NB:256, NB:256] = inv[1]
@@ -354,6 +348,20 @@
             return carry
 
         lax.fori_loop(p // 2 + 1, 4, solve, 0)
+
+        @pl.when(p == 0)
+        def _():
+            for_pair(1, stage_three)
+
+        @pl.when(p + 2 < PAIRS)
+        def _():
+            for_pair(p + 2, stage_two)
+
+        @pl.when(p + 4 < PAIRS)
+        def _():
+            for_pair(p + 4, stage_one)
+
+        own_copy(p).start()
 
     def own_step(p):
         @pl.when(is_giver & (p > 0))

time: 252 us -> 242 us (0.960)
  the two profiles are of different devices: /device:TPU:1 before, /device:TPU:4 now
where the time goes in v7:
time: 242 us
  Pallas kernels  234 us (97%)
  local copies, waits for them, and re-layouts  6.7 us (3%)
    pallas_call x1, Pallas kernels, local_part(): pl.pallas_call(body, out_shape=(jax.ShapeDtypeStruct(pan.shape, f32), jax...  211 us
    pallas_call x1, Pallas kernels, local_part(): pl.pallas_call(finish_body, grid=(8,), out_shape=(jax.ShapeDtypeStruct(tr...  22.7 us
    transpose x1, local copies, waits for them, and re-layouts, local_part(): pan = panel_tile.transpose(1, 0, 2).reshape(PAIRS, 3, 4, NB, NB)  6.7 us

profile of v7, /device:TPU:4, one launch (start us, length us, event | category | flops | bytes accessed | tf_op | source)
XLA Modules:
  0.0 241.5 jit_solution(8284818074467442154)
XLA Ops:
  0.6 6.7 %copy.4 = f32[8,1536,128]{2,1,0:T(8,128)} copy(f32[8,1536,128]{2,0,1:T(8,128)} %bitcast.4) | data formatting | bytes 12582912 | tf_op jit(solution)/shard_map/transpose | solution.py:503
  7.3 211.4 %factor.1 = (f32[8,3,4,128,128]{4,3,2,1,0:T(8,128)}, f32[8,1024,256]{2,1,0:T(8,128)}, f32[4,8,128,256]{3,2,1,0:T(8,128)}, f32[2,2,4,128,256]{4,3,2,1,0:T(8,128)}, f32[2,2,4,2,128,256]{5,4,3,2,1,0:T(8,128)}) custom-call(f32[8,3,4,128,128]{4,3,2,1,0:T(8,128)} %bitcast.3, f32[1536,2048]{1,0:T(8,128)} %trail.1), custom_call_target="tpu_custom_call" | custom-call | tf_op jit(solution)/shard_map/factor/pallas_call | solution.py:507
  218.8 22.7 %finish.1 = (f32[1536,2048]{1,0:T(8,128)}, f32[1536,8,128]{2,1,0:T(8,128)}) custom-call(f32[8,1024,256]{2,1,0:T(8,128)} %get-tuple-element.9.schur, f32[4,8,128,256]{3,2,1,0:T(8,128)} %get-tuple-element.10.top, f32[2,2,4,128,256]{4,3,2,1,0:T(8,128)} %get-tuple-element.11.left, f32[2,2,4,2,128,256]{5,4,3,2,1,0:T(8,128)} %get-tuple-element.12.right, ...), custom_call_target="tpu_custom_call" | custom-call | tf_op jit(solution)/shard_map/finish/pallas_call | solution.py:531

commit v8 on v7

--- a/solution.py
+++ b/solution.py
@@ -241,6 +241,17 @@
     def schur_update(q, b):
         schur[b] = schur[b] - dot_nt(own_rows(q), cols[q, b // 4, b % 4].reshape(256, 256))
 
+    def extra_update(p, e):
+        ahead = jnp.where(p < PAIRS - 1, p, 0)
+        is_lead = e < ahead
+        is_own = jnp.logical_not(is_lead) & (e - ahead < p - 1)
+        q = jnp.where(is_lead, e, jnp.where(is_own, e - ahead, 0))
+        right = jnp.where(is_lead, p + 1, jnp.where(is_own, p - 1, 0))
+        pair = jnp.where(is_lead, p + 1, jnp.where(is_own, p - 1, PAIRS))
+        rows = pl.ds(jnp.where(is_lead, 2, 4), 2)
+        value = work[pair, rows].reshape(1024, 256) - dot_nt(work[q, rows].reshape(1024, 256), rows256(q, right))
+        work[pair, rows] = value.reshape(2, 4, NB, 256)
+
     def factor(h, p):
         def store_upper(g, value):
             upper[8 * g:8 * g + 8, :] = value
@@ -260,15 +271,21 @@
             def beside(g):
                 if g % 4 == 0:
                     schur_update(p - LAG, 4 * h + g // 4)
+                elif g % 4 == 2 and g < 12:
+                    extra_update(p, 3 * h + g // 4)
 
             factor_block(load, store_upper, store_inv, beside)
 
         work[p, p // 2, 2 * (p % 2) + h, :, half(h)] = upper[...].T
 
     def lead_step(p):
-        @pl.when(p > 0)
+        @pl.when((p > 0) & (p <= LAG))
         def _():
             for_pair(p, lead_wait)
+
+        @pl.when((p >= LAG) & (p + 1 < PAIRS))
+        def _():
+            for_pair(p + 1, lead_wait)
 
         def subtract(q, carry):
             right = rows256(q, p)
@@ -279,7 +296,7 @@
 
             return lax.fori_loop(p // 2, 4, one, carry)
 
-        lax.fori_loop(0, p, subtract, 0)
+        lax.fori_loop((p - 1) * (p // 4), p, subtract, 0)
 
         @pl.when(p == LAG)
         def _():
@@ -293,8 +310,16 @@
         hi, lo = p // 2, 2 * (p % 2)
         diag[...] = work[p, hi, lo, :, 0:NB]
 
+        @pl.when(p > LAG)
+        def _():
+            own_wait(p - 1)
+
         def factor_half(h, carry):
             factor(h, p)
+
+            @pl.when((h == 0) & (p == LAG))
+            def _():
+                own_wait(p - 1)
 
             @pl.when(h == 0)
             def _():
@@ -310,9 +335,13 @@
                 for_pair(2, stage_one)
                 for_pair(3, stage_one)
 
-            @pl.when((h == 0) & (p > 0) & (p + 1 < PAIRS))
+            @pl.when((h == 0) & ((p == 1) | (p == 2)))
             def _():
                 for_pair(p + 1, stage_three)
+
+            @pl.when((h == 0) & (p >= 2) & (p + 2 < PAIRS))
+            def _():
+                for_pair(p + 2, stage_three)
 
             @pl.when(h == 0)
             def _():
@@ -353,15 +382,29 @@
         def _():
             for_pair(1, stage_three)
 
-        @pl.when(p + 2 < PAIRS)
+        @pl.when(p < 2)
         def _():
             for_pair(p + 2, stage_two)
 
+        @pl.when((p > 0) & (p + 3 < PAIRS))
+        def _():
+            for_pair(p + 3, stage_two)
+
         @pl.when(p + 4 < PAIRS)
         def _():
             for_pair(p + 4, stage_one)
 
-        own_copy(p).start()
+        @pl.when(p <= 2)
+        def _():
+            own_copy(p).start()
+
+        @pl.when((p >= 2) & (p + 1 < PAIRS))
+        def _():
+            own_copy(p + 1).start()
+
+    def own_wait(p):
+        keep_own(p).wait()
+        own_arrival(p).wait_recv()
 
     def own_step(p):
         @pl.when(is_giver & (p > 0))
@@ -369,14 +412,19 @@
             far_arrival(p - 1).wait_recv()
             pass_copy(p - 1).start()
 
-        keep_own(p).wait()
-        own_arrival(p).wait_recv()
+        @pl.when((p < LAG - 1) | (p == PAIRS - 1))
+        def _():
+            own_wait(p)
 
         def subtract(q, carry):
             set_own(p, own_rows(p) - dot_nt(own_rows(q), rows256(q, p)))
             return carry
 
-        lax.fori_loop(0, p, subtract, 0)
+        def reached(step):
+            return (p + 1 + 16 - step) // 16
+
+        done = 2 * reached(3) - reached(5) - reached(6) + 6 * reached(7) - 6 * reached(8)
+        lax.fori_loop(done, p, subtract, 0)
         set_own(p, dot_nt(own_rows(p), gmat[p % 2]))
 
         @pl.when(is_giver)
@@ -512,7 +560,7 @@
             in_specs=[any_spec] * 2,
             out_specs=(any_spec,) * 5,
             scratch_shapes=[
-                pltpu.VMEM((PAIRS, 6, 4, NB, 256), jnp.float32),
+                pltpu.VMEM((PAIRS + 1, 6, 4, NB, 256), jnp.float32),
                 pltpu.VMEM((PAIRS, 2, 4, 2, NB, 256), jnp.float32),
                 pltpu.VMEM((8, 1024, 256), jnp.float32),
                 pltpu.VMEM((NB, NB), jnp.float32),

time: 242 us -> 263 us (1.087)
  Pallas kernels: 234 us -> 255 us
    pallas_call x1, Pallas kernels: 211 us -> 233 us  [local_part(): pl.pallas_call(body, out_shape=(jax.ShapeDtypeStruct(pan.shape, f32), jax...]
where the time goes in v8:
time: 263 us
  Pallas kernels  255 us (97%)
  local copies, waits for them, and re-layouts  6.7 us (3%)
    pallas_call x1, Pallas kernels, local_part(): pl.pallas_call(body, out_shape=(jax.ShapeDtypeStruct(pan.shape, f32), jax...  233 us
    pallas_call x1, Pallas kernels, local_part(): pl.pallas_call(finish_body, grid=(8,), out_shape=(jax.ShapeDtypeStruct(tr...  22.7 us
    transpose x1, local copies, waits for them, and re-layouts, local_part(): pan = panel_tile.transpose(1, 0, 2).reshape(PAIRS, 3, 4, NB, NB)  6.7 us

profile of v8, /device:TPU:4, one launch (start us, length us, event | category | flops | bytes accessed | tf_op | source)
XLA Modules:
  0.0 262.8 jit_solution(119808446035530458)
XLA Ops:
  0.6 6.7 %copy.4 = f32[8,1536,128]{2,1,0:T(8,128)} copy(f32[8,1536,128]{2,0,1:T(8,128)} %bitcast.4) | data formatting | bytes 12582912 | tf_op jit(solution)/shard_map/transpose | solution.py:551
  7.3 232.7 %factor.1 = (f32[8,3,4,128,128]{4,3,2,1,0:T(8,128)}, f32[8,1024,256]{2,1,0:T(8,128)}, f32[4,8,128,256]{3,2,1,0:T(8,128)}, f32[2,2,4,128,256]{4,3,2,1,0:T(8,128)}, f32[2,2,4,2,128,256]{5,4,3,2,1,0:T(8,128)}) custom-call(f32[8,3,4,128,128]{4,3,2,1,0:T(8,128)} %bitcast.3, f32[1536,2048]{1,0:T(8,128)} %trail.1), custom_call_target="tpu_custom_call" | custom-call | tf_op jit(solution)/shard_map/factor/pallas_call | solution.py:555
  240.0 22.7 %finish.1 = (f32[1536,2048]{1,0:T(8,128)}, f32[1536,8,128]{2,1,0:T(8,128)}) custom-call(f32[8,1024,256]{2,1,0:T(8,128)} %get-tuple-element.9.schur, f32[4,8,128,256]{3,2,1,0:T(8,128)} %get-tuple-element.10.top, f32[2,2,4,128,256]{4,3,2,1,0:T(8,128)} %get-tuple-element.11.left, f32[2,2,4,2,128,256]{5,4,3,2,1,0:T(8,128)} %get-tuple-element.12.right, ...), custom_call_target="tpu_custom_call" | custom-call | tf_op jit(solution)/shard_map/finish/pallas_call | solution.py:579

commit v9 on v7

--- a/solution.py
+++ b/solution.py
@@ -251,18 +251,7 @@
         def load(i):
             return diag[8 * i:8 * i + 8, :]
 
-        @pl.when(p < LAG)
-        def _():
-            factor_block(load, store_upper, store_inv)
-
-        @pl.when(p >= LAG)
-        def _():
-            def beside(g):
-                if g % 4 == 0:
-                    schur_update(p - LAG, 4 * h + g // 4)
-
-            factor_block(load, store_upper, store_inv, beside)
-
+        factor_block(load, store_upper, store_inv)
         work[p, p // 2, 2 * (p % 2) + h, :, half(h)] = upper[...].T
 
     def lead_step(p):
@@ -289,6 +278,12 @@
         @pl.when(p >= LAG)
         def _():
             cols_wait(p - LAG)
+
+            def schur_step(b, carry):
+                schur_update(p - LAG, b)
+                return carry
+
+            lax.fori_loop(0, 8, schur_step, 0)
 
         hi, lo = p // 2, 2 * (p % 2)
         diag[...] = work[p, hi, lo, :, 0:NB]

time: 242 us -> 276 us (1.14)
  Pallas kernels: 234 us -> 268 us
    pallas_call x1, Pallas kernels: 211 us -> 246 us  [local_part(): pl.pallas_call(body, out_shape=(jax.ShapeDtypeStruct(pan.shape, f32), jax...]
where the time goes in v9:
time: 276 us
  Pallas kernels  268 us (97%)
  local copies, waits for them, and re-layouts  6.7 us (2%)
    pallas_call x1, Pallas kernels, local_part(): pl.pallas_call(body, out_shape=(jax.ShapeDtypeStruct(pan.shape, f32), jax...  246 us
    pallas_call x1, Pallas kernels, local_part(): pl.pallas_call(finish_body, grid=(8,), out_shape=(jax.ShapeDtypeStruct(tr...  22.7 us
    transpose x1, local copies, waits for them, and re-layouts, local_part(): pan = panel_tile.transpose(1, 0, 2).reshape(PAIRS, 3, 4, NB, NB)  6.7 us

profile of v9, /device:TPU:4, one launch (start us, length us, event | category | flops | bytes accessed | tf_op | source)
XLA Modules:
  0.0 275.8 jit_solution(286351438521054197)
XLA Ops:
  0.6 6.7 %copy.4 = f32[8,1536,128]{2,1,0:T(8,128)} copy(f32[8,1536,128]{2,0,1:T(8,128)} %bitcast.4) | data formatting | bytes 12582912 | tf_op jit(solution)/shard_map/transpose | solution.py:498
  7.3 245.7 %factor.1 = (f32[8,3,4,128,128]{4,3,2,1,0:T(8,128)}, f32[8,1024,256]{2,1,0:T(8,128)}, f32[4,8,128,256]{3,2,1,0:T(8,128)}, f32[2,2,4,128,256]{4,3,2,1,0:T(8,128)}, f32[2,2,4,2,128,256]{5,4,3,2,1,0:T(8,128)}) custom-call(f32[8,3,4,128,128]{4,3,2,1,0:T(8,128)} %bitcast.3, f32[1536,2048]{1,0:T(8,128)} %trail.1), custom_call_target="tpu_custom_call" | custom-call | tf_op jit(solution)/shard_map/factor/pallas_call | solution.py:502
  253.1 22.7 %finish.1 = (f32[1536,2048]{1,0:T(8,128)}, f32[1536,8,128]{2,1,0:T(8,128)}) custom-call(f32[8,1024,256]{2,1,0:T(8,128)} %get-tuple-element.9.schur, f32[4,8,128,256]{3,2,1,0:T(8,128)} %get-tuple-element.10.top, f32[2,2,4,128,256]{4,3,2,1,0:T(8,128)} %get-tuple-element.11.left, f32[2,2,4,2,128,256]{5,4,3,2,1,0:T(8,128)} %get-tuple-element.12.right, ...), custom_call_target="tpu_custom_call" | custom-call | tf_op jit(solution)/shard_map/finish/pallas_call | solution.py:526

commit v10 on v7

--- a/solution.py
+++ b/solution.py
@@ -73,7 +73,7 @@
         store_inv(g, jnp.where(lane < base + 8, cur, 0.0) * scale)
 
 
-def body(pan, trail, pan_out, schur_out, top_out, left_out, right_out, work, cols, schur, diag, upper, inv, gmat, top, zero,
+def body(pan, raw, trail, pan_out, schur_out, top_out, left_out, right_out, work, cols, schur, diag, upper, inv, gmat, top, zero, stage,
          lead_sem, lead_send, lead_recv, own_sem, own_send, own_recv, keep_sem, give_send, give_recv, pass_send,
          far_send, far_recv, in_sem, out_sem, top_sem, left_sem, pan_sem):
     my_row = lax.axis_index("pr")
@@ -115,7 +115,7 @@
 
     def mine(part):
         p, lo, hi, _ = part
-        return pan.at[p, 0, lo:hi]
+        return pan.at[p, lo:hi]
 
     def keep_strip(part):
         return pltpu.make_async_copy(mine(part), strip(part, my_row, my_col), lead_sem.at[part[3]])
@@ -169,14 +169,21 @@
         for kind in range(7):
             lead_copy(part, kind).wait_send()
 
-    def keep_own(p):
-        return pltpu.make_async_copy(pan.at[p, 1:3], work.at[p, 4:6, :, :, half(my_col)], own_sem.at[p])
+    def own_load():
+        return pltpu.make_async_copy(raw.at[pl.ds(512, 1024)], stage, own_sem.at[0])
+
+    def spread_own():
+        flat = stage.reshape(1024 * PAIRS, NB)
+        for p in range(PAIRS):
+            work[p, 4:6, :, :, half(my_col)] = flat[pl.ds(p, 1024, stride=PAIRS), :].reshape(2, 4, NB, NB)
 
     def own_copy(p):
-        return remote(pan.at[p, 1:3], work.at[p, 4:6, :, :, half(my_col)], own_send.at[p], own_recv.at[p], across)
+        there = work.at[p, 4:6, :, :, half(my_col)]
+        return remote(there, there, own_send.at[p], own_recv.at[p], across)
 
     def own_arrival(p):
-        return remote(pan.at[p, 1:3], work.at[p, 4:6, :, :, half(1 - my_col)], own_send.at[p], own_recv.at[p], across)
+        there = work.at[p, 4:6, :, :, half(1 - my_col)]
+        return remote(there, there, own_send.at[p], own_recv.at[p], across)
 
     def keep_copy(p):
         return pltpu.make_async_copy(work.at[p, 4:6], cols.at[p, :, :, chip], keep_sem.at[p])
@@ -236,6 +243,7 @@
     stage_one(second_part)
     for_pair(1, stage_one)
     stage_three(first_part)
+    own_load().start()
     lead_wait(first_part)
 
     def schur_update(q, b):
@@ -314,9 +322,10 @@
             def _():
                 for_pair(p + 1, stage_three)
 
-            @pl.when(h == 0)
-            def _():
-                keep_own(p).start()
+            @pl.when((h == 0) & (p == 0))
+            def _():
+                own_load().wait()
+                spread_own()
 
             @pl.when((h == 0) & (p == 1))
             def _():
@@ -364,13 +373,13 @@
         own_copy(p).start()
 
     def own_step(p):
-        @pl.when(is_giver & (p > 0))
+        @pl.when(is_giver & (p > 0) & (p < PAIRS - 1))
         def _():
             far_arrival(p - 1).wait_recv()
             pass_copy(p - 1).start()
 
-        keep_own(p).wait()
         own_arrival(p).wait_recv()
+        own_copy(p).wait_send()
 
         def subtract(q, carry):
             set_own(p, own_rows(p) - dot_nt(own_rows(q), rows256(q, p)))
@@ -452,6 +461,11 @@
         return carry
 
     lax.fori_loop(0, 8, tail, 0)
+
+    @pl.when(is_giver)
+    def _():
+        far_arrival(PAIRS - 2).wait_recv()
+        pass_copy(PAIRS - 2).start()
 
     for r in range(3):
         top_rows(r)
@@ -474,8 +488,6 @@
     pltpu.make_async_copy(pan_out, pan_out, pan_sem.at[0]).wait()
 
     def finish(p, carry):
-        own_copy(p).wait_send()
-
         @pl.when(is_giver)
         def _():
             give_copy(p).wait_send()
@@ -500,16 +512,16 @@
 
 def solution(mesh):
     def local_part(panel_tile, trail_tile):
-        pan = panel_tile.transpose(1, 0, 2).reshape(PAIRS, 3, 4, NB, NB)
+        pan = panel_tile[:512].transpose(1, 0, 2).reshape(PAIRS, 4, NB, NB)
         any_spec = pl.BlockSpec(memory_space=pl.ANY)
         dma = pltpu.SemaphoreType.DMA
         f32 = jnp.float32
         pan_out, schur, top, left, right = pl.pallas_call(
             body,
-            out_shape=(jax.ShapeDtypeStruct(pan.shape, f32), jax.ShapeDtypeStruct((8, 1024, 256), f32),
+            out_shape=(jax.ShapeDtypeStruct((PAIRS, 3, 4, NB, NB), f32), jax.ShapeDtypeStruct((8, 1024, 256), f32),
                        jax.ShapeDtypeStruct((4, 8, NB, 256), f32), jax.ShapeDtypeStruct((LAST, 2, 4, NB, 256), f32),
                        jax.ShapeDtypeStruct((LAST, 2, 4, 2, NB, 256), f32)),
-            in_specs=[any_spec] * 2,
+            in_specs=[any_spec] * 3,
             out_specs=(any_spec,) * 5,
             scratch_shapes=[
                 pltpu.VMEM((PAIRS, 6, 4, NB, 256), jnp.float32),
@@ -521,13 +533,14 @@
                 pltpu.VMEM((2, 256, 256), jnp.float32),
                 pltpu.VMEM((2, 8, NB, 256), jnp.float32),
                 pltpu.VMEM((NB, NB), jnp.float32),
+                pltpu.VMEM((1024, PAIRS, NB), jnp.float32),
                 dma((PAIRS + 1,)), dma((PAIRS + 1, 7)), dma((PAIRS + 1, 7)), dma((PAIRS,)), dma((PAIRS,)), dma((PAIRS,)), dma((PAIRS,)),
                 dma((PAIRS,)), dma((PAIRS,)), dma((PAIRS,)), dma((PAIRS,)), dma((PAIRS,)), dma((8,)), dma((8,)), dma((2,)), dma((2,)),
                 dma((1,)),
             ],
             compiler_params=pltpu.CompilerParams(collective_id=0, has_side_effects=True, vmem_limit_bytes=64 * 1024 * 1024 - 65536),
             name="factor",
-        )(pan, trail_tile)
+        )(pan, panel_tile, trail_tile)
         trail_out, panel_out = pl.pallas_call(
             finish_body,
             grid=(8,),

time: 242 us -> 229 us (0.946)
  Pallas kernels: 234 us -> 224 us
  local copies, waits for them, and re-layouts: 6.7 us -> 3.43 us
    pallas_call x1, Pallas kernels: 211 us -> 202 us  [local_part(): pl.pallas_call(body, out_shape=(jax.ShapeDtypeStruct((PAIRS, 3, 4, NB, NB...]
    transpose x1 -> x2, local copies, waits for them, and re-layouts: 6.7 us -> 3.43 us  [local_part(): pan = panel_tile[:512].transpose(1, 0, 2).reshape(PAIRS, 4, NB, NB)]
where the time goes in v10:
time: 229 us; the launch traced here: 228 us
  Pallas kernels  224 us (98%)
  local copies, waits for them, and re-layouts  3.43 us (1%)
    pallas_call x1, Pallas kernels, local_part(): pl.pallas_call(body, out_shape=(jax.ShapeDtypeStruct((PAIRS, 3, 4, NB, NB...  202 us
    pallas_call x1, Pallas kernels, local_part(): pl.pallas_call(finish_body, grid=(8,), out_shape=(jax.ShapeDtypeStruct(tr...  22.7 us

profile of v10, /device:TPU:4, one launch (start us, length us, event | category | flops | bytes accessed | tf_op | source)
XLA Modules:
  0.0 228.3 jit_solution(10385520723069517244)
XLA Ops:
  0.6 1.7 slice_bitcast_fusion
  2.4 1.7 copy.4
  4.1 201.5 %factor.1 = (f32[8,3,4,128,128]{4,3,2,1,0:T(8,128)}, f32[8,1024,256]{2,1,0:T(8,128)}, f32[4,8,128,256]{3,2,1,0:T(8,128)}, f32[2,2,4,128,256]{4,3,2,1,0:T(8,128)}, f32[2,2,4,2,128,256]{5,4,3,2,1,0:T(8,128)}) custom-call(f32[8,4,128,128]{3,2,1,0:T(8,128)} %bitcast.4, f32[1536,8,128]{2,1,0:T(8,128)} %raw.1, f32[1536,2048]{1,0:T(8,128)} %trail.1), custom_call_target="tpu_custom_call" | custom-call | tf_op jit(solution)/shard_map/factor/pallas_call | solution.py:519
  205.6 22.7 %finish.1 = (f32[1536,2048]{1,0:T(8,128)}, f32[1536,8,128]{2,1,0:T(8,128)}) custom-call(f32[8,1024,256]{2,1,0:T(8,128)} %get-tuple-element.9.schur, f32[4,8,128,256]{3,2,1,0:T(8,128)} %get-tuple-element.10.top, f32[2,2,4,128,256]{4,3,2,1,0:T(8,128)} %get-tuple-element.11.left, f32[2,2,4,2,128,256]{5,4,3,2,1,0:T(8,128)} %get-tuple-element.12.right, ...), custom_call_target="tpu_custom_call" | custom-call | tf_op jit(solution)/shard_map/finish/pallas_call | solution.py:544
